TPU v7x, 256 devices: a whole 4x4x8 slice. The times are simulated.
256 devices in a mesh: rows: 32 (over y, x, core), cols: 8 (over z).
Axes of the slice: x: 4, y: 4, z: 8, core: 2. Of those that a mesh axis runs over, the one named last changes fastest.
Arguments:
- grads: bfloat16 [8192, 4096], P('rows', 'cols'), may hold values from -6 to 6
- probe: bfloat16 [8192, 4096], P('rows', 'cols'), may hold values from -6 to 6
- left_factor: float32 [8192], P('rows'), may hold values from 0.5 to 2
- q_right: float32 [4096, 4096], P('cols', 'rows'), may hold values from -1 to 2
- q_inv_t: float32 [4096, 4096], P('cols', 'rows'), may hold values from -1 to 2
Outputs:
- left_new: float32 [8192], P('rows')
- q_new: float32 [4096, 4096], P('cols', 'rows')
All inputs are finite; a program needn't handle non-finite values. Where the computation divides by a largest or mean magnitude, that divisor is 1e-20 or more.
Results may differ from a plain program's by a relative error of at most 0.0058.
Values may be sent and summed in bfloat16 or wider, within the bound.
No kernel may reach another device: no remote copies, remote signals or barrier semaphores. Data moves between devices by JAX's collectives and lax.ppermute only.
A program may use at most 64 MiB of HBM per device.

v0:
```python
import jax
import jax.numpy as jnp
from jax import lax
from jax.experimental.layout import Layout, with_layout_constraint
from jax.sharding import Mesh
from jax.sharding import PartitionSpec as P

ROWS = ("rows_0", "rows_1", "rows_2")
PLANE = ("rows_0", "rows_1")
CORE = "rows_2"
COLS = "cols"


learn_rate = 0.2
epsilon = 1e-06
NOTE_ROWS = 16
f32 = jnp.float32
bf16 = jnp.bfloat16


def shift(value, axis, by):
    size = lax.axis_size(axis)
    return lax.ppermute(value, axis, [(i, (i + by) % size) for i in range(size)])


def ring_gather(value, axis, put, result, half_dim):
    size, me = lax.axis_size(axis), lax.axis_index(axis)
    result = put(result, value, me, 0)
    up = down = value
    for step in range(1, size // 2):
        up, down = shift(up, axis, 1), shift(down, axis, -1)
        result = put(result, up, (me - step + size) % size, 0)
        result = put(result, down, (me + step) % size, 0)
    half = value.shape[half_dim] // 2
    first = lax.slice_in_dim(up, 0, half, axis=half_dim)
    second = lax.slice_in_dim(down, half, 2 * half, axis=half_dim)
    opposite = (me + size // 2) % size
    result = put(result, shift(first, axis, 1), opposite, 0)
    return put(result, shift(second, axis, -1), opposite, half)


def gather_plane(value, first, second):
    n_0, n_1 = (lax.axis_size(axis) for axis in PLANE)

    def put_line(line, block, owner, row):
        return lax.dynamic_update_slice(line, block[None], (owner, row, 0))

    def put_plane(plane, block, owner, begin):
        if second == PLANE[0]:
            return lax.dynamic_update_slice(plane, block[None], (owner, begin, 0, 0))
        return lax.dynamic_update_slice(plane, block[:, None], (begin, owner, 0, 0))

    line = jnp.zeros((lax.axis_size(first), *value.shape), value.dtype)
    size, me = lax.axis_size(first), lax.axis_index(first)
    line = put_line(line, value, me, 0)
    for by in (1, -1, 2):
        line = put_line(line, shift(value, first, by), (me - by + size) % size, 0)
    plane = jnp.zeros((n_0, n_1, *value.shape), value.dtype)
    return ring_gather(line, second, put_plane, plane, 0)


def from_everyone(value, axes):
    size = lax.axis_size(axes)
    copies = jnp.broadcast_to(value[None], (size, *value.shape))
    return lax.all_to_all(copies, axes, 0, 0, tiled=True)


def dot(left, right, left_dim, right_dim):
    return lax.dot_general(
        left, right, (((left_dim,), (right_dim,)), ((), ())), preferred_element_type=f32
    )


def turned(values, by):
    size = values.shape[0]
    twice = jnp.concatenate([values, values], axis=0)
    return lax.dynamic_slice_in_dim(twice, (by + size) % size, size, axis=0)


def split(value):
    high = lax.reduce_precision(value, 8, 7)
    middle = lax.reduce_precision(value - high, 8, 7)
    return [t.astype(bf16) for t in (high, middle, value - high - middle)]


def after(values, *others):
    return lax.optimization_barrier((values, *others))[0]


def body(grads, probe, left_factor, q_right, q_inv_t):
    n_cols, me = lax.axis_size(COLS), lax.axis_index(COLS)
    core = lax.axis_index(CORE)
    n_plane = lax.axis_size(PLANE)
    height, width = grads.shape
    half = width // 2
    piece = half // n_plane

    q_low = q_right.astype(bf16)
    inv_low = q_inv_t.astype(bf16)
    both = lax.all_gather(jnp.concatenate([grads, probe], axis=0), COLS, axis=1, tiled=True)

    def half_of(value, which):
        return lax.dynamic_slice_in_dim(value, which * half, half, axis=1)

    def in_core_order(mine, others, axis):
        first = jnp.concatenate([mine, others], axis=axis)
        second = jnp.concatenate([others, mine], axis=axis)
        return jnp.where(core == 0, first, second)

    q_t, inv_t = q_low.T, inv_low.T
    got = shift(jnp.concatenate([half_of(q_t, 1 - core), half_of(inv_t, 1 - core)], axis=1), CORE, 1)
    q_pair = in_core_order(half_of(q_t, core), got[:, :half], 0)
    inv_pair = in_core_order(half_of(inv_t, core), got[:, half:], 0)
    q_half = gather_plane(q_pair, "rows_1", "rows_0").reshape(-1, half)
    inv_half = gather_plane(inv_pair, "rows_0", "rows_1").reshape(-1, half)
    q_other, inv_other = shift(q_half, CORE, 1), shift(inv_half, CORE, 1)

    def whitened(scale, values, mine, others):
        parts = [(scale[:, None] * dot(values, q, 1, 0)).astype(bf16) for q in (mine, others)]
        return in_core_order(*parts, 1)

    white = whitened(left_factor, both[:height], q_half, q_other)
    conj = whitened(1.0 / left_factor, both[height:], inv_half, inv_other)

    own = jnp.concatenate([white, conj], axis=0)
    before, behind = shift(own, COLS, 1), shift(own, COLS, -1)
    before_2 = shift(before, COLS, 1)
    behind_2 = shift(behind, COLS, -1)

    def pair(left, right):
        signed = jnp.concatenate([right[:height], -right[height:]], axis=0)
        return with_layout_constraint(dot(left, signed, 0, 0), Layout(major_to_minor=(0, 1)))

    def over_cores(pairs):
        products = []
        for a, b in pairs:
            products.append(pair(a, b))
        part = jnp.concatenate(products, axis=1)
        keep = lax.dynamic_slice_in_dim(part, core * half, half, axis=0)
        give = lax.dynamic_slice_in_dim(part, (1 - core) * half, half, axis=0).astype(bf16)
        got = shift(give, CORE, 1)
        part = (keep + got.astype(f32)).astype(bf16)
        return part.reshape(n_plane, piece, part.shape[1])

    def over_plane(part):
        parts = lax.all_to_all(part, PLANE, 0, 0, tiled=True)
        return jnp.sum(parts.astype(f32), axis=0)

    early_part = over_cores([(own, own), (own, behind), (before, behind)])
    early = over_plane(early_part)
    before_2, behind_2, white, conj, _ = lax.optimization_barrier(
        (before_2, behind_2, white, conj, early_part)
    )
    late_part = over_cores([(before, behind_2), (before_2, behind_2)])
    late = over_plane(late_part)

    white_f, conj_f = white.astype(f32), conj.astype(f32)
    left_part = jnp.sum(white_f * white_f - conj_f * conj_f, axis=1)
    q_all = lax.all_gather(after(q_low, late_part), COLS, axis=0, tiled=True)

    top_r = jnp.maximum(jnp.max(jnp.abs(early)), jnp.max(jnp.abs(late)))
    d0, d1, d2 = (early[:, i * width : (i + 1) * width].astype(bf16) for i in range(3))
    d3, d4 = (late[:, i * width : (i + 1) * width].astype(bf16) for i in range(2))
    way = ((jnp.arange(n_cols) - me + n_cols) % n_cols)[:, None, None]

    def by_way(choices):
        out = jnp.zeros((n_cols, *d0.shape), bf16)
        for i, value in choices.items():
            out = jnp.where(way == i % n_cols, value[None], out)
        return out

    sent = [by_way({1: d1, -1: d2, 2: d3, -2: d4}), by_way({1: d2, -1: d3})]
    terms = split(jnp.concatenate([left_part, jnp.full((128,), top_r)]))
    note = jnp.concatenate([t.reshape(-1, 128) for t in terms], axis=0)
    note = jnp.pad(note, ((0, NOTE_ROWS - note.shape[0]), (0, 0)))
    note = note.reshape(piece, -1)
    note = jnp.broadcast_to(note[None], (n_cols, *note.shape))
    blocks = lax.all_to_all(
        jnp.concatenate([*sent, note], axis=2), COLS, 0, 0, tiled=True
    )

    def got(by, size):
        block = lax.dynamic_index_in_dim(blocks, (me + by + n_cols) % n_cols, 0, keepdims=False)
        return block[:, :size]

    above, above_2 = got(1, 2 * width), got(2, width)
    below, below_2 = got(-1, 2 * width), got(-2, width)
    slices = jnp.concatenate([d0, d1, above, above_2, below, below_2], axis=1)
    gram = lax.all_gather(slices, (CORE, *PLANE), axis=0, tiled=True)

    lines = height // 128 + 1
    notes = blocks[:, :, 2 * width :].reshape(n_cols, NOTE_ROWS, 128).astype(f32)
    notes = (notes[:, :lines] + notes[:, lines : 2 * lines]) + notes[:, 2 * lines : 3 * lines]
    left_grad = jnp.sum(notes[:, :-1].reshape(n_cols, -1), axis=0)
    tops = jnp.stack([jnp.max(notes[:, -1]), jnp.max(jnp.abs(left_grad))])
    tops = from_everyone(jnp.broadcast_to(tops[:, None, None], (2, 8, 128)), ROWS)
    top_r, top_l = jnp.max(tops[:, 0]), jnp.max(tops[:, 1])
    scale_r = learn_rate / (top_r + epsilon)
    scale_l = learn_rate / (top_l + epsilon)
    left_new = left_factor - scale_l * left_grad * left_factor

    q_near = turned(q_all.reshape(n_cols, width, -1), me).reshape(n_cols * width, -1)
    ahead = 5 * width
    product = dot(gram[:, :ahead], q_near[:ahead], 1, 0)
    for i in range(3):
        at = (n_cols - 1 - i) * width
        block = gram[:, ahead + i * width : ahead + (i + 1) * width]
        product = product + dot(block, q_near[at : at + width], 0, 0)
    q_new = q_right - scale_r * product
    return (left_new, q_new)


def solution(mesh):
    finer = Mesh(
        mesh.devices.reshape(4, 4, 2, mesh.shape["cols"]), ("rows_0", "rows_1", "rows_2", "cols")
    )
    in_specs = (P(ROWS, "cols"), P(ROWS, "cols"), P(ROWS), P("cols", ROWS), P("cols", ROWS))
    out_specs = (P(ROWS), P("cols", ROWS))

    return jax.shard_map(body, mesh=finer, in_specs=in_specs, out_specs=out_specs, check_vma=False)
```

profile of v0, /device:TPU:2, one launch (start us, length us, event | category | flops | bytes accessed | tf_op | source)
XLA Modules:
  0.0 227.8 jit_solution(5811077225392120624)
XLA Ops:
  14.3 2.0 collective-permute-start.3
  23.9 2.1 collective-permute-start.5
  26.6 3.9 %collective-permute-start.12 = (bf16[4,256,256]{2,1,0:T(8,128)(2,1)S(1)}, bf16[4,256,256]{2,1,0:T(8,128)(2,1)}, u32[]{:S(2)}, u32[]{:S(2)}) collective-permute-start(bf16[4,256,256]{2,1,0:T(8,128)(2,1)S(1)} %bitcast_dynamic-update-slice_fusion.10), channel_id=1, source_target_pairs={{0,16},{16,32},{32,48},{48,0},{1,17},{17,33},{33,49},{49,1},{2,18}... | collective-permute-start | bytes 1572872 | tf_op jit(solution)/shard_map/ppermute | solution.py:23
  33.2 4.6 %collective-permute-done.4 = bf16[4,256,256]{2,1,0:T(8,128)(2,1)} collective-permute-done((bf16[4,256,256]{2,1,0:T(8,128)(2,1)S(1)}, bf16[4,256,256]{2,1,0:T(8,128)(2,1)}, u32[]{:S(2)}, u32[]{:S(2)}) %collective-permute-start.4) | collective-permute-done | bytes 524320 | tf_op jit(solution)/shard_map/ppermute | solution.py:23
  40.1 3.1 %collective-permute-start.7 = (bf16[2,256,256]{2,1,0:T(8,128)(2,1)S(1)}, bf16[2,256,256]{2,1,0:T(8,128)(2,1)S(1)}, u32[]{:S(2)}, u32[]{:S(2)}) collective-permute-start(bf16[2,256,256]{2,1,0:T(8,128)(2,1)S(1)} %slice.177), channel_id=1, source_target_pairs={{0,192},{64,0},{128,64},{192,128},{1,193},{65,1},{129,65},{193,129... | collective-permute-start | bytes 786440 | tf_op jit(solution)/shard_map/ppermute | solution.py:23
  55.6 11.9 %all-gather.4.cloned.1.call-done = bf16[512,4096]{1,0:T(8,128)(2,1)} async-done(((bf16[512,512]{1,0:T(8,128)(2,1)}), bf16[512,4096]{1,0:T(8,128)(2,1)}) %all-gather.4.cloned.1.call-update) | async-done | bytes 4194320 | tf_op jit(solution)/shard_map/all_gather | solution.py:100
  67.5 3.3 %fusion.33 = bf16[256,256]{0,1:T(8,128)(2,1)S(1)} fusion(bf16[4096,256]{1,0:T(8,128)(2,1)} %bitcast.14, bf16[512,4096]{1,0:T(8,128)(2,1)} %all-gather.4.cloned.1.call-done, f32[256]{0:T(256)S(1)} %copy-done.4), kind=kOutput, calls=%fused_computation.32 | convolution fusion | flops 537001984 | bytes 4326400 | tf_op jit(solution)/shard_map/dot_general | solution.py:69
  71.0 2.6 %fusion.30 = bf16[256,256]{0,1:T(8,128)(2,1)S(1)} fusion(bf16[4096,256]{1,0:T(8,128)(2,1)} %collective-permute-done.8, bf16[512,4096]{1,0:T(8,128)(2,1)S(1)} %copy-done.5, f32[256]{0:T(256)S(1)} %copy-done.4), kind=kOutput, calls=%fused_computation.31 | convolution fusion | flops 537001984 | bytes 4326400 | tf_op jit(solution)/shard_map/dot_general | solution.py:69
  74.7 2.6 %fusion.24 = bf16[256,256]{0,1:T(8,128)(2,1)S(1)} fusion(bf16[4096,256]{1,0:T(8,128)(2,1)} %collective-permute-done.16, bf16[512,4096]{1,0:T(8,128)(2,1)S(1)} %copy-done.5, f32[256]{0:T(256)S(1)} %broadcast_divide_fusion), kind=kOutput, calls=%fused_computation.29 | convolution fusion | flops 537001984 | bytes 4326400 | tf_op jit(solution)/shard_map/dot_general | solution.py:69
  80.0 11.0 %collective-permute-done.19 = bf16[512,512]{0,1:T(8,128)(2,1)S(1)} collective-permute-done((bf16[512,512]{0,1:T(8,128)(2,1)S(1)}, bf16[512,512]{0,1:T(8,128)(2,1)S(1)}, u32[]{:S(2)}, u32[]{:S(2)}) %collective-permute-start.19) | collective-permute-done | bytes 524320 | tf_op jit(solution)/shard_map/ppermute | solution.py:23
  94.3 3.2 %collective-permute-start.20 = (bf16[512,512]{0,1:T(8,128)(2,1)S(1)}, bf16[512,512]{0,1:T(8,128)(2,1)S(1)}, u32[]{:S(2)}, u32[]{:S(2)}) collective-permute-start(bf16[512,512]{0,1:T(8,128)(2,1)S(1)} %collective-permute-done.19), channel_id=1, source_target_pairs={{0,7},{1,0},{2,1},{3,2},{4,3},{5,4},{6,5},{7,6},{8,15},{9,8},{10,9... | collective-permute-start | bytes 1572872 | tf_op jit(solution)/shard_map/ppermute | solution.py:23
  98.6 11.1 %collective-permute-done.18 = bf16[512,512]{0,1:T(8,128)(2,1)S(1)} collective-permute-done((bf16[512,512]{0,1:T(8,128)(2,1)S(1)}, bf16[512,512]{0,1:T(8,128)(2,1)S(1)}, u32[]{:S(2)}, u32[]{:S(2)}) %collective-permute-start.18) | collective-permute-done | bytes 524320 | tf_op jit(solution)/shard_map/ppermute | solution.py:23
  111.6 7.2 %all-to-all-start.1 = ((bf16[16,16,1536]{2,1,0:T(8,128)(2,1)}), bf16[16,16,1536]{2,1,0:T(8,128)(2,1)S(1)}, u32[]{:S(2)}, u32[]{:S(2)}) async-start(bf16[16,16,1536]{2,1,0:T(8,128)(2,1)} %bitcast.103), calls=%async_computation.1 | async-start | bytes 1572864 | tf_op jit(solution)/shard_map/all_to_all | solution.py:146
  119.1 2.0 fusion.41
  121.2 11.4 %all-to-all-done.1 = bf16[16,16,1536]{2,1,0:T(8,128)(2,1)S(1)} async-done(((bf16[16,16,1536]{2,1,0:T(8,128)(2,1)}), bf16[16,16,1536]{2,1,0:T(8,128)(2,1)S(1)}, u32[]{:S(2)}, u32[]{:S(2)}) %all-to-all-start.1) | async-done | bytes 786464 | tf_op jit(solution)/shard_map/all_to_all | solution.py:146
  132.6 5.0 %all-to-all-start = ((bf16[16,16,1024]{2,1,0:T(8,128)(2,1)}), bf16[16,16,1024]{2,1,0:T(8,128)(2,1)S(1)}, u32[]{:S(2)}, u32[]{:S(2)}) async-start(bf16[16,16,1024]{2,1,0:T(8,128)(2,1)} %bitcast.34), calls=%async_computation | async-start | bytes 1048576 | tf_op jit(solution)/shard_map/all_to_all | solution.py:146
  138.3 9.1 %all-to-all-done = bf16[16,16,1024]{2,1,0:T(8,128)(2,1)S(1)} async-done(((bf16[16,16,1024]{2,1,0:T(8,128)(2,1)}), bf16[16,16,1024]{2,1,0:T(8,128)(2,1)S(1)}, u32[]{:S(2)}, u32[]{:S(2)}) %all-to-all-start) | async-done | bytes 524320 | tf_op jit(solution)/shard_map/all_to_all | solution.py:146
  150.2 5.8 %all-to-all-start.2 = ((bf16[8,16,1152]{2,1,0:T(8,128)(2,1)}), bf16[8,16,1152]{2,1,0:T(8,128)(2,1)S(1)}, u32[]{:S(2)}, u32[]{:S(2)}) async-start(bf16[8,16,1152]{2,1,0:T(8,128)(2,1)} %pad_maximum_fusion.11), calls=%async_computation.2 | async-start | bytes 589824 | tf_op jit(solution)/shard_map/all_to_all | solution.py:178
  156.2 10.8 %all-to-all-done.2 = bf16[8,16,1152]{2,1,0:T(8,128)(2,1)S(1)} async-done(((bf16[8,16,1152]{2,1,0:T(8,128)(2,1)}), bf16[8,16,1152]{2,1,0:T(8,128)(2,1)S(1)}, u32[]{:S(2)}, u32[]{:S(2)}) %all-to-all-start.2) | async-done | bytes 294944 | tf_op jit(solution)/shard_map/all_to_all | solution.py:178
  171.1 5.6 %all-to-all-start.3 = ((f32[32,2,8,128]{3,2,1,0:T(8,128)}), f32[32,2,8,128]{3,2,1,0:T(8,128)S(1)}, u32[]{:S(2)}, u32[]{:S(2)}) async-start(f32[32,2,8,128]{3,2,1,0:T(8,128)} %broadcast_in_dim_broadcast_in_dim_broadcast_in_dim.2), calls=%async_computation.3 | async-start | bytes 524288 | tf_op jit(solution)/shard_map/all_to_all | solution.py:65
  176.8 8.2 %all-to-all-done.3 = f32[32,2,8,128]{3,2,1,0:T(8,128)S(1)} async-done(((f32[32,2,8,128]{3,2,1,0:T(8,128)}), f32[32,2,8,128]{3,2,1,0:T(8,128)S(1)}, u32[]{:S(2)}, u32[]{:S(2)}) %all-to-all-start.3) | async-done | bytes 262176 | tf_op jit(solution)/shard_map/all_to_all | solution.py:65
  189.6 24.2 %all-gather.6.cloned.1.call-done = bf16[512,4096]{1,0:T(8,128)(2,1)} async-done(((bf16[16,4096]{1,0:T(8,128)(2,1)}), bf16[512,4096]{1,0:T(8,128)(2,1)}) %all-gather.6.cloned.1.call-update) | async-done | bytes 4194320 | tf_op jit(solution)/shard_map/all_gather | solution.py:189
  213.8 2.6 %fusion = f32[512,128]{1,0:T(8,128)S(1)} fusion(bf16[2560,128]{1,0:T(8,128)(2,1)S(1)} %bitcast.106, bf16[512,4096]{1,0:T(8,128)(2,1)} %all-gather.6.cloned.1.call-done), kind=kOutput, calls=%fused_computation.1 | convolution fusion | flops 335544320 | bytes 3538944 | tf_op jit(solution)/shard_map/dot_general | solution.py:69
  219.2 2.1 fusion.11
  (142 shorter events, 55.3 us)
Async XLA Ops:
  7.2 60.3 %all-gather.4.cloned.1.call-start = ((), (), s32[]{:S(2)}) async-start(), calls=%async_computation.4 | async-start | bytes 4718592 | tf_op jit(solution)/shard_map/all_gather | solution.py:100
  13.5 8.3 %collective-permute-start.2 = (bf16[256,256]{1,0:T(8,128)(2,1)S(1)}, bf16[256,256]{1,0:T(8,128)(2,1)S(1)}, u32[]{:S(2)}, u32[]{:S(2)}) collective-permute-start(bf16[256,256]{1,0:T(8,128)(2,1)S(1)} %maximum_select_fusion.3), channel_id=1, source_target_pairs={{0,48},{16,0},{32,16},{48,32},{1,49},{17,1},{33,17},{49,33},{2,50}... | collective-permute-start | bytes 393224 | tf_op jit(solution)/shard_map/ppermute | solution.py:23
  14.3 8.3 %collective-permute-start.3 = (bf16[256,256]{1,0:T(8,128)(2,1)S(1)}, bf16[256,256]{1,0:T(8,128)(2,1)S(1)}, u32[]{:S(2)}, u32[]{:S(2)}) collective-permute-start(bf16[256,256]{1,0:T(8,128)(2,1)S(1)} %maximum_select_fusion.3), channel_id=1, source_target_pairs={{0,32},{16,48},{32,0},{48,16},{1,33},{17,49},{33,1},{49,17},{2,34}... | collective-permute-start | bytes 393224 | tf_op jit(solution)/shard_map/ppermute | solution.py:23
  16.3 9.6 %collective-permute-start.9 = (bf16[256,256]{1,0:T(8,128)(2,1)S(1)}, bf16[256,256]{1,0:T(8,128)(2,1)S(1)}, u32[]{:S(2)}, u32[]{:S(2)}) collective-permute-start(bf16[256,256]{1,0:T(8,128)(2,1)S(1)} %maximum_select_fusion.5), channel_id=1, source_target_pairs={{0,64},{64,128},{128,192},{192,0},{1,65},{65,129},{129,193},{193,1... | collective-permute-start | bytes 393224 | tf_op jit(solution)/shard_map/ppermute | solution.py:23
  17.8 8.2 %collective-permute-start.10 = (bf16[256,256]{1,0:T(8,128)(2,1)S(1)}, bf16[256,256]{1,0:T(8,128)(2,1)S(1)}, u32[]{:S(2)}, u32[]{:S(2)}) collective-permute-start(bf16[256,256]{1,0:T(8,128)(2,1)S(1)} %maximum_select_fusion.5), channel_id=1, source_target_pairs={{0,192},{64,0},{128,64},{192,128},{1,193},{65,1},{129,65},{193,129... | collective-permute-start | bytes 393224 | tf_op jit(solution)/shard_map/ppermute | solution.py:23
  22.7 15.2 %collective-permute-start.4 = (bf16[4,256,256]{2,1,0:T(8,128)(2,1)S(1)}, bf16[4,256,256]{2,1,0:T(8,128)(2,1)}, u32[]{:S(2)}, u32[]{:S(2)}) collective-permute-start(bf16[4,256,256]{2,1,0:T(8,128)(2,1)S(1)} %bitcast_dynamic-update-slice_fusion.13), channel_id=1, source_target_pairs={{0,64},{64,128},{128,192},{192,0},{1,65},{65,129},{129,193},{193,1... | collective-permute-start | bytes 1572872 | tf_op jit(solution)/shard_map/ppermute | solution.py:23
  23.9 15.2 %collective-permute-start.5 = (bf16[4,256,256]{2,1,0:T(8,128)(2,1)S(1)}, bf16[4,256,256]{2,1,0:T(8,128)(2,1)}, u32[]{:S(2)}, u32[]{:S(2)}) collective-permute-start(bf16[4,256,256]{2,1,0:T(8,128)(2,1)S(1)} %bitcast_dynamic-update-slice_fusion.13), channel_id=1, source_target_pairs={{0,192},{64,0},{128,64},{192,128},{1,193},{65,1},{129,65},{193,129... | collective-permute-start | bytes 1572872 | tf_op jit(solution)/shard_map/ppermute | solution.py:23
  26.6 16.5 %collective-permute-start.12 = (bf16[4,256,256]{2,1,0:T(8,128)(2,1)S(1)}, bf16[4,256,256]{2,1,0:T(8,128)(2,1)}, u32[]{:S(2)}, u32[]{:S(2)}) collective-permute-start(bf16[4,256,256]{2,1,0:T(8,128)(2,1)S(1)} %bitcast_dynamic-update-slice_fusion.10), channel_id=1, source_target_pairs={{0,16},{16,32},{32,48},{48,0},{1,17},{17,33},{33,49},{49,1},{2,18}... | collective-permute-start | bytes 1572872 | tf_op jit(solution)/shard_map/ppermute | solution.py:23
  30.5 15.3 %collective-permute-start.13 = (bf16[4,256,256]{2,1,0:T(8,128)(2,1)S(1)}, bf16[4,256,256]{2,1,0:T(8,128)(2,1)}, u32[]{:S(2)}, u32[]{:S(2)}) collective-permute-start(bf16[4,256,256]{2,1,0:T(8,128)(2,1)S(1)} %bitcast_dynamic-update-slice_fusion.10), channel_id=1, source_target_pairs={{0,48},{16,0},{32,16},{48,32},{1,49},{17,1},{33,17},{49,33},{2,50}... | collective-permute-start | bytes 1572872 | tf_op jit(solution)/shard_map/ppermute | solution.py:23
  38.8 12.5 %collective-permute-start.6 = (bf16[2,256,256]{2,1,0:T(8,128)(2,1)S(1)}, bf16[2,256,256]{2,1,0:T(8,128)(2,1)S(1)}, u32[]{:S(2)}, u32[]{:S(2)}) collective-permute-start(bf16[2,256,256]{2,1,0:T(8,128)(2,1)S(1)} %slice.176), channel_id=1, source_target_pairs={{0,64},{64,128},{128,192},{192,0},{1,65},{65,129},{129,193},{193,1... | collective-permute-start | bytes 786440 | tf_op jit(solution)/shard_map/ppermute | solution.py:23
  40.1 11.9 %collective-permute-start.7 = (bf16[2,256,256]{2,1,0:T(8,128)(2,1)S(1)}, bf16[2,256,256]{2,1,0:T(8,128)(2,1)S(1)}, u32[]{:S(2)}, u32[]{:S(2)}) collective-permute-start(bf16[2,256,256]{2,1,0:T(8,128)(2,1)S(1)} %slice.177), channel_id=1, source_target_pairs={{0,192},{64,0},{128,64},{192,128},{1,193},{65,1},{129,65},{193,129... | collective-permute-start | bytes 786440 | tf_op jit(solution)/shard_map/ppermute | solution.py:23
  44.1 10.8 %collective-permute-start.14 = (bf16[2,256,256]{2,1,0:T(8,128)(2,1)S(1)}, bf16[2,256,256]{2,1,0:T(8,128)(2,1)S(1)}, u32[]{:S(2)}, u32[]{:S(2)}) collective-permute-start(bf16[2,256,256]{2,1,0:T(8,128)(2,1)S(1)} %slice.180), channel_id=1, source_target_pairs={{0,16},{16,32},{32,48},{48,0},{1,17},{17,33},{33,49},{49,1},{2,18}... | collective-permute-start | bytes 786440 | tf_op jit(solution)/shard_map/ppermute | solution.py:23
  52.7 18.1 %collective-permute-start.8 = (bf16[4096,256]{1,0:T(8,128)(2,1)}, bf16[4096,256]{1,0:T(8,128)(2,1)}, u32[]{:S(2)}, u32[]{:S(2)}) collective-permute-start(bf16[4096,256]{1,0:T(8,128)(2,1)} %bitcast.14), channel_id=1, source_target_pairs={{0,8},{8,0},{1,9},{9,1},{2,10},{10,2},{3,11},{11,3},{4,12},{12,4},... | collective-permute-start | bytes 6291464 | tf_op jit(solution)/shard_map/ppermute | solution.py:23
  55.0 19.7 %collective-permute-start.16 = (bf16[4096,256]{1,0:T(8,128)(2,1)S(1)}, bf16[4096,256]{1,0:T(8,128)(2,1)}, u32[]{:S(2)}, u32[]{:S(2)}) collective-permute-start(bf16[4096,256]{1,0:T(8,128)(2,1)S(1)} %bitcast.104), channel_id=1, source_target_pairs={{0,8},{8,0},{1,9},{9,1},{2,10},{10,2},{3,11},{11,3},{4,12},{12,4},... | collective-permute-start | bytes 6291464 | tf_op jit(solution)/shard_map/ppermute | solution.py:23
  77.4 13.6 %collective-permute-start.19 = (bf16[512,512]{0,1:T(8,128)(2,1)S(1)}, bf16[512,512]{0,1:T(8,128)(2,1)S(1)}, u32[]{:S(2)}, u32[]{:S(2)}) collective-permute-start(bf16[512,512]{0,1:T(8,128)(2,1)S(1)} %pad_maximum_fusion.2), channel_id=1, source_target_pairs={{0,7},{1,0},{2,1},{3,2},{4,3},{5,4},{6,5},{7,6},{8,15},{9,8},{10,9... | collective-permute-start | bytes 1572872 | tf_op jit(solution)/shard_map/ppermute | solution.py:23
  78.9 14.4 %collective-permute-start.17 = (bf16[512,512]{0,1:T(8,128)(2,1)S(1)}, bf16[512,512]{0,1:T(8,128)(2,1)S(1)}, u32[]{:S(2)}, u32[]{:S(2)}) collective-permute-start(bf16[512,512]{0,1:T(8,128)(2,1)S(1)} %pad_maximum_fusion.2), channel_id=1, source_target_pairs={{0,1},{1,2},{2,3},{3,4},{4,5},{5,6},{6,7},{7,0},{8,9},{9,10},{10,1... | collective-permute-start | bytes 1572872 | tf_op jit(solution)/shard_map/ppermute | solution.py:23
  94.2 15.5 %collective-permute-start.18 = (bf16[512,512]{0,1:T(8,128)(2,1)S(1)}, bf16[512,512]{0,1:T(8,128)(2,1)S(1)}, u32[]{:S(2)}, u32[]{:S(2)}) collective-permute-start(bf16[512,512]{0,1:T(8,128)(2,1)S(1)} %collective-permute-done.17), channel_id=1, source_target_pairs={{0,1},{1,2},{2,3},{3,4},{4,5},{5,6},{6,7},{7,0},{8,9},{9,10},{10,1... | collective-permute-start | bytes 1572872 | tf_op jit(solution)/shard_map/ppermute | solution.py:23
  94.3 15.4 %collective-permute-start.20 = (bf16[512,512]{0,1:T(8,128)(2,1)S(1)}, bf16[512,512]{0,1:T(8,128)(2,1)S(1)}, u32[]{:S(2)}, u32[]{:S(2)}) collective-permute-start(bf16[512,512]{0,1:T(8,128)(2,1)S(1)} %collective-permute-done.19), channel_id=1, source_target_pairs={{0,7},{1,0},{2,1},{3,2},{4,3},{5,4},{6,5},{7,6},{8,15},{9,8},{10,9... | collective-permute-start | bytes 1572872 | tf_op jit(solution)/shard_map/ppermute | solution.py:23
  111.6 21.0 %all-to-all-start.1 = ((bf16[16,16,1536]{2,1,0:T(8,128)(2,1)}), bf16[16,16,1536]{2,1,0:T(8,128)(2,1)S(1)}, u32[]{:S(2)}, u32[]{:S(2)}) async-start(bf16[16,16,1536]{2,1,0:T(8,128)(2,1)} %bitcast.103), calls=%async_computation.1 | async-start | bytes 1572864 | tf_op jit(solution)/shard_map/all_to_all | solution.py:146
  118.9 68.7 %all-gather.8.cloned.1.call-start = ((), (), s32[]{:S(2)}) async-start(), calls=%async_computation.6 | async-start | bytes 1179648 | tf_op jit(solution)/shard_map/all_gather | solution.py:159
  132.6 14.8 %all-to-all-start = ((bf16[16,16,1024]{2,1,0:T(8,128)(2,1)}), bf16[16,16,1024]{2,1,0:T(8,128)(2,1)S(1)}, u32[]{:S(2)}, u32[]{:S(2)}) async-start(bf16[16,16,1024]{2,1,0:T(8,128)(2,1)} %bitcast.34), calls=%async_computation | async-start | bytes 1048576 | tf_op jit(solution)/shard_map/all_to_all | solution.py:146
  150.2 16.7 %all-to-all-start.2 = ((bf16[8,16,1152]{2,1,0:T(8,128)(2,1)}), bf16[8,16,1152]{2,1,0:T(8,128)(2,1)S(1)}, u32[]{:S(2)}, u32[]{:S(2)}) async-start(bf16[8,16,1152]{2,1,0:T(8,128)(2,1)} %pad_maximum_fusion.11), calls=%async_computation.2 | async-start | bytes 589824 | tf_op jit(solution)/shard_map/all_to_all | solution.py:178
  156.1 57.8 %all-gather.6.cloned.1.call-start = ((), (), s32[]{:S(2)}) async-start(), calls=%async_computation.5 | async-start | bytes 4325376 | tf_op jit(solution)/shard_map/all_gather | solution.py:189
  171.1 13.9 %all-to-all-start.3 = ((f32[32,2,8,128]{3,2,1,0:T(8,128)}), f32[32,2,8,128]{3,2,1,0:T(8,128)S(1)}, u32[]{:S(2)}, u32[]{:S(2)}) async-start(f32[32,2,8,128]{3,2,1,0:T(8,128)} %broadcast_in_dim_broadcast_in_dim_broadcast_in_dim.2), calls=%async_computation.3 | async-start | bytes 524288 | tf_op jit(solution)/shard_map/all_to_all | solution.py:65
  (12 other events, 61.8 us)
Sparse Core Ops, SparseCore 0:
  9.8 57.6 all-gather.3
  121.5 39.5 all-gather.7
  167.8 45.9 all-gather.5
where the time goes:
time: 231 us; the launch traced here: 228 us
  waiting for transfers between devices  107 us (46%)
  starting transfers between devices  52.6 us (23%)
  matrix products  19.2 us (8%)
  local copies, waits for them, and re-layouts  18.8 us (8%)
  between operations  17.2 us (7%)
  other arithmetic  13.3 us (6%)
    ppermute x23, waiting for transfers between devices, shift(): lax.ppermute(value, axis, [(i, (i + by) % size) for i in range(size)])  31.2 us
    ppermute x23, starting transfers between devices, shift(): lax.ppermute(value, axis, [(i, (i + by) % size) for i in range(size)])  28.8 us
    all_gather x1, waiting for transfers between devices, body(): gram = lax.all_gather(slices, (CORE, *PLANE), axis=0, tiled=True)  24.2 us
    all_to_all x2, waiting for transfers between devices, over_plane(): parts = lax.all_to_all(part, PLANE, 0, 0, tiled=True)  20.5 us
    dot_general x13, matrix products, dot(): lax.dot_general(left, right, (((left_dim,), (right_dim,)), ((), ())), pre...  19.2 us
    all_to_all x2, starting transfers between devices, over_plane(): parts = lax.all_to_all(part, PLANE, 0, 0, tiled=True)  12.2 us
    all_gather x1, waiting for transfers between devices, body(): lax.all_gather(jnp.concatenate([grads, probe], axis=0), COLS, axis=1, til...  11.9 us
    all_to_all x1, waiting for transfers between devices, body(): lax.all_to_all(jnp.concatenate([*sent, note], axis=2), COLS, 0, 0, tiled=...  10.8 us
  transfers between devices with their start and end apart: 30, of which 13 were waited for; matrix products, arithmetic and copies ran while one was open for 16% of the time, Pallas kernels for 0%

commit v1 on v0

--- a/solution.py
+++ b/solution.py
@@ -1,7 +1,9 @@
 import jax
 import jax.numpy as jnp
 from jax import lax
+from jax.experimental import pallas as pl
 from jax.experimental.layout import Layout, with_layout_constraint
+from jax.experimental.pallas import tpu as pltpu
 from jax.sharding import Mesh
 from jax.sharding import PartitionSpec as P
 
@@ -13,7 +15,6 @@
 
 learn_rate = 0.2
 epsilon = 1e-06
-NOTE_ROWS = 16
 f32 = jnp.float32
 bf16 = jnp.bfloat16
 
@@ -71,20 +72,55 @@
     )
 
 
-def turned(values, by):
-    size = values.shape[0]
-    twice = jnp.concatenate([values, values], axis=0)
-    return lax.dynamic_slice_in_dim(twice, (by + size) % size, size, axis=0)
-
-
 def split(value):
     high = lax.reduce_precision(value, 8, 7)
     middle = lax.reduce_precision(value - high, 8, 7)
     return [t.astype(bf16) for t in (high, middle, value - high - middle)]
 
 
-def after(values, *others):
-    return lax.optimization_barrier((values, *others))[0]
+def whitened_kernel(core_ref, scale_ref, both_ref, q_ref, q_other_ref, inv_ref, inv_other_ref, out_ref, sums):
+    step = pl.program_id(0)
+    rows, columns = out_ref.shape[0] // 2, out_ref.shape[1] // 2
+
+    @pl.when(step == 0)
+    def _():
+        sums[...] = jnp.zeros_like(sums)
+
+    for i, refs in enumerate(((q_ref, q_other_ref), (inv_ref, inv_other_ref))):
+        values = both_ref[i * rows : (i + 1) * rows, :]
+        for j, ref in enumerate(refs):
+            sums[j, i * rows : (i + 1) * rows, :] += jnp.dot(
+                values, ref[...], preferred_element_type=f32
+            )
+
+    @pl.when(step == pl.num_programs(0) - 1)
+    def _():
+        mine, others = (scale_ref[...] * sums[j] for j in range(2))
+        first = core_ref[0] == 0
+        out_ref[:, :columns] = jnp.where(first, mine, others).astype(out_ref.dtype)
+        out_ref[:, columns:] = jnp.where(first, others, mine).astype(out_ref.dtype)
+
+
+def whitened(core, scale, both, *factors):
+    (rows, depth), half = both.shape, factors[0].shape[1]
+    deep = min(512, depth)
+    return pl.pallas_call(
+        whitened_kernel,
+        grid=(depth // deep,),
+        out_shape=jax.ShapeDtypeStruct((rows, 2 * half), bf16),
+        in_specs=[
+            pl.BlockSpec(memory_space=pltpu.SMEM),
+            pl.BlockSpec((rows, 1), lambda k: (0, 0)),
+            pl.BlockSpec((rows, deep), lambda k: (0, k)),
+            *[pl.BlockSpec((deep, half), lambda k: (k, 0)) for _ in factors],
+        ],
+        out_specs=pl.BlockSpec((rows, 2 * half), lambda k: (0, 0)),
+        scratch_shapes=[pltpu.VMEM((2, rows, half), f32)],
+        cost_estimate=pl.CostEstimate(
+            flops=4 * rows * depth * half, bytes_accessed=2 * depth * (rows + 4 * half), transcendentals=0
+        ),
+        name="whitened",
+    )(core[None], scale, both, *factors)
 
 
 def body(grads, probe, left_factor, q_right, q_inv_t):
@@ -115,15 +151,12 @@
     inv_half = gather_plane(inv_pair, "rows_0", "rows_1").reshape(-1, half)
     q_other, inv_other = shift(q_half, CORE, 1), shift(inv_half, CORE, 1)
 
-    def whitened(scale, values, mine, others):
-        parts = [(scale[:, None] * dot(values, q, 1, 0)).astype(bf16) for q in (mine, others)]
-        return in_core_order(*parts, 1)
-
-    white = whitened(left_factor, both[:height], q_half, q_other)
-    conj = whitened(1.0 / left_factor, both[height:], inv_half, inv_other)
-
-    own = jnp.concatenate([white, conj], axis=0)
-    before, behind = shift(own, COLS, 1), shift(own, COLS, -1)
+    scale = jnp.concatenate([left_factor, 1.0 / left_factor])[:, None]
+    own = whitened(core, scale, both, q_half, q_other, inv_half, inv_other)
+    white, conj = own[:height], own[height:]
+
+    before = shift(own, COLS, 1)
+    behind = shift(own, COLS, -1)
     before_2 = shift(before, COLS, 1)
     behind_2 = shift(behind, COLS, -1)
 
@@ -146,66 +179,67 @@
         parts = lax.all_to_all(part, PLANE, 0, 0, tiled=True)
         return jnp.sum(parts.astype(f32), axis=0)
 
-    early_part = over_cores([(own, own), (own, behind), (before, behind)])
+    early_part = over_cores([(own, own), (own, behind)])
     early = over_plane(early_part)
-    before_2, behind_2, white, conj, _ = lax.optimization_barrier(
-        (before_2, behind_2, white, conj, early_part)
-    )
-    late_part = over_cores([(before, behind_2), (before_2, behind_2)])
-    late = over_plane(late_part)
-
     white_f, conj_f = white.astype(f32), conj.astype(f32)
     left_part = jnp.sum(white_f * white_f - conj_f * conj_f, axis=1)
-    q_all = lax.all_gather(after(q_low, late_part), COLS, axis=0, tiled=True)
+    strip = q_low.shape[1]
+    lines = height // strip
+    terms = jnp.stack(split(left_part)).reshape(3 * lines, strip)
+    terms = jnp.pad(terms, ((0, 16 - 3 * lines), (0, 0)))
+    q_all = lax.all_gather(jnp.concatenate([q_low, terms], axis=0), COLS, axis=0, tiled=True)
+    q_all = q_all.reshape(n_cols, width + 16, -1)
+    terms = q_all[:, width : width + 3 * lines].astype(f32).reshape(n_cols, 3, height)
+    left_grad = jnp.sum((terms[:, 0] + terms[:, 1]) + terms[:, 2], axis=0)
+    top_l = jnp.max(jnp.abs(left_grad))
+    before_2, behind_2, _ = lax.optimization_barrier((before_2, behind_2, early_part))
+    late_part = over_cores([(before, behind), (before, behind_2), (before_2, behind_2)])
+    late = over_plane(late_part)
+
 
     top_r = jnp.maximum(jnp.max(jnp.abs(early)), jnp.max(jnp.abs(late)))
-    d0, d1, d2 = (early[:, i * width : (i + 1) * width].astype(bf16) for i in range(3))
-    d3, d4 = (late[:, i * width : (i + 1) * width].astype(bf16) for i in range(2))
-    way = ((jnp.arange(n_cols) - me + n_cols) % n_cols)[:, None, None]
-
-    def by_way(choices):
-        out = jnp.zeros((n_cols, *d0.shape), bf16)
-        for i, value in choices.items():
-            out = jnp.where(way == i % n_cols, value[None], out)
-        return out
-
-    sent = [by_way({1: d1, -1: d2, 2: d3, -2: d4}), by_way({1: d2, -1: d3})]
-    terms = split(jnp.concatenate([left_part, jnp.full((128,), top_r)]))
-    note = jnp.concatenate([t.reshape(-1, 128) for t in terms], axis=0)
-    note = jnp.pad(note, ((0, NOTE_ROWS - note.shape[0]), (0, 0)))
-    note = note.reshape(piece, -1)
-    note = jnp.broadcast_to(note[None], (n_cols, *note.shape))
-    blocks = lax.all_to_all(
-        jnp.concatenate([*sent, note], axis=2), COLS, 0, 0, tiled=True
-    )
-
-    def got(by, size):
-        block = lax.dynamic_index_in_dim(blocks, (me + by + n_cols) % n_cols, 0, keepdims=False)
-        return block[:, :size]
-
-    above, above_2 = got(1, 2 * width), got(2, width)
-    below, below_2 = got(-1, 2 * width), got(-2, width)
-    slices = jnp.concatenate([d0, d1, above, above_2, below, below_2], axis=1)
-    gram = lax.all_gather(slices, (CORE, *PLANE), axis=0, tiled=True)
-
-    lines = height // 128 + 1
-    notes = blocks[:, :, 2 * width :].reshape(n_cols, NOTE_ROWS, 128).astype(f32)
-    notes = (notes[:, :lines] + notes[:, lines : 2 * lines]) + notes[:, 2 * lines : 3 * lines]
-    left_grad = jnp.sum(notes[:, :-1].reshape(n_cols, -1), axis=0)
-    tops = jnp.stack([jnp.max(notes[:, -1]), jnp.max(jnp.abs(left_grad))])
-    tops = from_everyone(jnp.broadcast_to(tops[:, None, None], (2, 8, 128)), ROWS)
-    top_r, top_l = jnp.max(tops[:, 0]), jnp.max(tops[:, 1])
+    terms = jnp.stack(split(jnp.stack([top_r, top_l]))).reshape(1, 6)
+    note = jnp.broadcast_to(jnp.pad(terms, ((0, 0), (0, 122))), (piece, 128))
+    pieces = jnp.concatenate([early.astype(bf16), late.astype(bf16), note], axis=1)
+    mine = from_everyone(pieces, PLANE).reshape(half, -1)
+    gram = in_core_order(mine, shift(mine, CORE, 1), 0)
+
+    def joined(terms):
+        terms = terms.astype(f32)
+        return (terms[:, 0] + terms[:, 1]) + terms[:, 2]
+
+    top_r, top_l = jnp.max(joined(gram[:, 5 * width : 5 * width + 6].reshape(width, 3, 2)), axis=0)
+    top_r = jnp.full((8, 128), top_r)
+    top_r = jnp.maximum(top_r, shift(top_r, COLS, n_cols // 2))[0, 0]
+
+    def block(i, size=1):
+        return gram[:, i * width : (i + size) * width]
+
+    def q_at(by, size=1):
+        rows = [
+            lax.dynamic_index_in_dim(q_all, (me + by + i + n_cols) % n_cols, 0, keepdims=False)[:width]
+            for i in range(size)
+        ]
+        return jnp.concatenate(rows, axis=0)
+
+    note = jnp.pad(jnp.stack(split(top_r))[:, None], ((0, 13), (0, strip - 1)))
+
+    def sent(value, by):
+        return shift(jnp.concatenate([value.astype(bf16), note], axis=0), COLS, by)
+
+    got = [
+        sent(dot(block(4), q_at(2), 1, 0), -2),
+        sent(dot(block(3), q_at(-1), 0, 0), 2),
+        sent(dot(block(2, 2), q_at(1, 2), 1, 0), -1),
+        sent(dot(block(1), q_at(0), 0, 0) + dot(block(2), q_at(-1), 0, 0), 1),
+    ]
+    product = dot(block(0, 2), q_at(0, 2), 1, 0)
+    for value in got:
+        product = product + value[:width].astype(f32)
+        top_r = jnp.maximum(top_r, joined(value[width : width + 3, :1].T)[0])
     scale_r = learn_rate / (top_r + epsilon)
     scale_l = learn_rate / (top_l + epsilon)
     left_new = left_factor - scale_l * left_grad * left_factor
-
-    q_near = turned(q_all.reshape(n_cols, width, -1), me).reshape(n_cols * width, -1)
-    ahead = 5 * width
-    product = dot(gram[:, :ahead], q_near[:ahead], 1, 0)
-    for i in range(3):
-        at = (n_cols - 1 - i) * width
-        block = gram[:, ahead + i * width : ahead + (i + 1) * width]
-        product = product + dot(block, q_near[at : at + width], 0, 0)
     q_new = q_right - scale_r * product
     return (left_new, q_new)
 

time: 231 us -> 234 us (1.013)
  waiting for transfers between devices: 107 us -> 62.6 us
  blocking collectives: 0 us -> 23.3 us
  between operations: 17.2 us -> 29.3 us
  Pallas kernels: 0 us -> 9.33 us
  matrix products: 19.2 us -> 13.9 us
  other arithmetic: 13.3 us -> 18.5 us
  local copies, waits for them, and re-layouts: 18.8 us -> 23.4 us
    all_gather x2 -> x1, waiting for transfers between devices: 24.2 us -> 0.01 us  [body(): lax.all_gather(jnp.concatenate([q_low, terms], axis=0), COLS, axis=0, til...]
    all_to_all x0 -> x1, blocking collectives: none -> 23.3 us  [from_everyone(): return lax.all_to_all(copies, axes, 0, 0, tiled=True)]
    all_to_all x2 -> x0, waiting for transfers between devices: 19 us -> none  [the longest x1 10.8 us: body(): lax.all_to_all(jnp.concatenate([*sent, note], axis=2), COLS, 0, 0, tiled=...]
    all_to_all x2 -> x0, starting transfers between devices: 11.5 us -> none  [the longest x1 5.83 us: body(): lax.all_to_all(jnp.concatenate([*sent, note], axis=2), COLS, 0, 0, tiled=...]
    ppermute x23 -> x29, starting transfers between devices: 28.8 us -> 38.1 us  [shift(): lax.ppermute(value, axis, [(i, (i + by) % size) for i in range(size)])]
    pallas_call x0 -> x1, Pallas kernels: none -> 9.33 us  [whitened(): pl.pallas_call(whitened_kernel, grid=(depth // deep,), out_shape=jax.Shap...]
    ppermute x23 -> x29, waiting for transfers between devices: 31.2 us -> 38.3 us  [shift(): lax.ppermute(value, axis, [(i, (i + by) % size) for i in range(size)])]
    all_gather x1, waiting for transfers between devices: 11.9 us -> 5.39 us  [body(): lax.all_gather(jnp.concatenate([grads, probe], axis=0), COLS, axis=1, til...]
  transfers between devices with their start and end apart: 30 -> 33, of which waited for: 13 -> 13; matrix products, arithmetic and copies ran while one was open for 16% -> 18% of each run, Pallas kernels for 0% -> 0%
where the time goes in v1:
time: 234 us; the launch traced here: 231 us
  waiting for transfers between devices  62.6 us (27%)
  starting transfers between devices  51.1 us (22%)
  between operations  29.3 us (13%)
  local copies, waits for them, and re-layouts  23.4 us (10%)
  blocking collectives  23.3 us (10%)
  other arithmetic  18.5 us (8%)
  matrix products  13.9 us (6%)
  Pallas kernels  9.33 us (4%)
    ppermute x29, waiting for transfers between devices, shift(): lax.ppermute(value, axis, [(i, (i + by) % size) for i in range(size)])  38.3 us
    ppermute x29, starting transfers between devices, shift(): lax.ppermute(value, axis, [(i, (i + by) % size) for i in range(size)])  38.1 us
    all_to_all x1, blocking collectives, from_everyone(): return lax.all_to_all(copies, axes, 0, 0, tiled=True)  23.3 us
    all_to_all x2, waiting for transfers between devices, over_plane(): parts = lax.all_to_all(part, PLANE, 0, 0, tiled=True)  18.9 us
    dot_general x11, matrix products, dot(): lax.dot_general(left, right, (((left_dim,), (right_dim,)), ((), ())), pre...  13.9 us
    all_to_all x2, starting transfers between devices, over_plane(): parts = lax.all_to_all(part, PLANE, 0, 0, tiled=True)  12.8 us
    pallas_call x1, Pallas kernels, whitened(): pl.pallas_call(whitened_kernel, grid=(depth // deep,), out_shape=jax.Shap...  9.33 us
    dynamic_update_slice x5, local copies, waits for them, and re-layouts, put_plane(): return lax.dynamic_update_slice(plane, block[:, None], (begin, owner, 0, 0))  6.07 us
  transfers between devices with their start and end apart: 33, of which 13 were waited for; matrix products, arithmetic and copies ran while one was open for 18% of the time, Pallas kernels for 0%

profile of v1, /device:TPU:2, one launch (start us, length us, event | category | flops | bytes accessed | tf_op | source)
XLA Modules:
  0.0 231.4 jit_solution(2836078986894674666)
XLA Ops:
  15.2 2.0 collective-permute-start.11
  19.7 2.2 collective-permute-start.3
  27.8 2.7 %collective-permute-start.5 = (bf16[4,256,256]{2,1,0:T(8,128)(2,1)S(1)}, bf16[4,256,256]{2,1,0:T(8,128)(2,1)}, u32[]{:S(2)}, u32[]{:S(2)}) collective-permute-start(bf16[4,256,256]{2,1,0:T(8,128)(2,1)S(1)} %constant_dynamic-update-slice_fusion.4), channel_id=1, source_target_pairs={{0,192},{64,0},{128,64},{192,128},{1,193},{65,1},{129,65},{193,129... | collective-permute-start | bytes 1572872 | tf_op jit(solution)/shard_map/ppermute | solution.py:24
  33.2 4.4 %collective-permute-done.12 = bf16[4,256,256]{2,1,0:T(8,128)(2,1)} collective-permute-done((bf16[4,256,256]{2,1,0:T(8,128)(2,1)S(1)}, bf16[4,256,256]{2,1,0:T(8,128)(2,1)}, u32[]{:S(2)}, u32[]{:S(2)}) %collective-permute-start.12) | collective-permute-done | bytes 524320 | tf_op jit(solution)/shard_map/ppermute | solution.py:24
  44.5 2.7 %collective-permute-start.7 = (bf16[2,256,256]{2,1,0:T(8,128)(2,1)S(1)}, bf16[2,256,256]{2,1,0:T(8,128)(2,1)S(1)}, u32[]{:S(2)}, u32[]{:S(2)}) collective-permute-start(bf16[2,256,256]{2,1,0:T(8,128)(2,1)S(1)} %slice.233), channel_id=1, source_target_pairs={{0,192},{64,0},{128,64},{192,128},{1,193},{65,1},{129,65},{193,129... | collective-permute-start | bytes 786440 | tf_op jit(solution)/shard_map/ppermute | solution.py:24
  56.2 2.9 %collective-permute-done.16.inv_other_ref = bf16[4096,256]{1,0:T(8,128)(2,1)} collective-permute-done((bf16[4096,256]{1,0:T(8,128)(2,1)}, bf16[4096,256]{1,0:T(8,128)(2,1)}, u32[]{:S(2)}, u32[]{:S(2)}) %collective-permute-start.16) | collective-permute-done | bytes 2097184 | tf_op jit(solution)/shard_map/ppermute | solution.py:24
  59.1 3.0 %collective-permute-done.8.q_other_ref = bf16[4096,256]{1,0:T(8,128)(2,1)} collective-permute-done((bf16[4096,256]{1,0:T(8,128)(2,1)S(1)}, bf16[4096,256]{1,0:T(8,128)(2,1)}, u32[]{:S(2)}, u32[]{:S(2)}) %collective-permute-start.8) | collective-permute-done | bytes 2097184 | tf_op jit(solution)/shard_map/ppermute | solution.py:24
  62.1 5.4 %all-gather.3.cloned.1.call-done.both_ref = bf16[512,4096]{1,0:T(8,128)(2,1)} async-done(((bf16[512,512]{1,0:T(8,128)(2,1)}), bf16[512,4096]{1,0:T(8,128)(2,1)}) %all-gather.3.cloned.1.call-update) | async-done | bytes 4194320 | tf_op jit(solution)/shard_map/all_gather | solution.py:136
  67.5 9.3 %whitened.1 = bf16[512,512]{1,0:T(8,128)(2,1)} custom-call(s32[1]{0:T(128)} %bitcast.core_ref, f32[512,1]{1,0:T(8,128)} %copy.61.scale_ref, bf16[512,4096]{1,0:T(8,128)(2,1)} %all-gather.3.cloned.1.call-done.both_ref, bf16[4096,256]{1,0:T(8,128)(2,1)} %bitcast.101, bf16[4096,256]{1,0:T(8,128)(2,1)} %collective-permute-done.8.q_other_ref, ...), custom_call_target="tpu_custom_call" | custom-call | flops 2147483648 | bytes 12582912 | tf_op jit(solution)/shard_map/whitened/pallas_call | solution.py:107
  82.7 7.9 %collective-permute-done.17 = bf16[512,512]{1,0:T(8,128)(2,1)S(1)} collective-permute-done((bf16[512,512]{1,0:T(8,128)(2,1)}, bf16[512,512]{1,0:T(8,128)(2,1)S(1)}, u32[]{:S(2)}, u32[]{:S(2)}) %collective-permute-start.17) | collective-permute-done | bytes 524320 | tf_op jit(solution)/shard_map/ppermute | solution.py:24
  92.0 2.6 %collective-permute-start.21 = (bf16[512,512]{1,0:T(8,128)(2,1)S(1)}, bf16[512,512]{1,0:T(8,128)(2,1)S(1)}, u32[]{:S(2)}, u32[]{:S(2)}) collective-permute-start(bf16[512,512]{1,0:T(8,128)(2,1)S(1)} %collective-permute-done.17), channel_id=1, source_target_pairs={{0,7},{1,0},{2,1},{3,2},{4,3},{5,4},{6,5},{7,6},{8,15},{9,8},{10,9... | collective-permute-start | bytes 1572872 | tf_op jit(solution)/shard_map/ppermute | solution.py:24
  98.9 11.3 %collective-permute-done.20 = bf16[512,512]{1,0:T(8,128)(2,1)} collective-permute-done((bf16[512,512]{1,0:T(8,128)(2,1)}, bf16[512,512]{1,0:T(8,128)(2,1)}, u32[]{:S(2)}, u32[]{:S(2)}) %collective-permute-start.20) | collective-permute-done | bytes 524320 | tf_op jit(solution)/shard_map/ppermute | solution.py:24
  114.5 8.0 %all-to-all-start = ((bf16[16,16,1024]{2,1,0:T(8,128)(2,1)}), bf16[16,16,1024]{2,1,0:T(8,128)(2,1)}, u32[]{:S(2)}, u32[]{:S(2)}) async-start(bf16[16,16,1024]{2,1,0:T(8,128)(2,1)} %bitcast.104), calls=%async_computation | async-start | bytes 1048576 | tf_op jit(solution)/shard_map/all_to_all | solution.py:179
  122.5 2.2 add_convert_fusion
  124.7 9.1 %all-to-all-done = bf16[16,16,1024]{2,1,0:T(8,128)(2,1)} async-done(((bf16[16,16,1024]{2,1,0:T(8,128)(2,1)}), bf16[16,16,1024]{2,1,0:T(8,128)(2,1)}, u32[]{:S(2)}, u32[]{:S(2)}) %all-to-all-start) | async-done | bytes 524320 | tf_op jit(solution)/shard_map/all_to_all | solution.py:179
  133.8 4.9 %all-to-all-start.1 = ((bf16[16,16,1536]{2,1,0:T(8,128)(2,1)}), bf16[16,16,1536]{2,1,0:T(8,128)(2,1)S(1)}, u32[]{:S(2)}, u32[]{:S(2)}) async-start(bf16[16,16,1536]{2,1,0:T(8,128)(2,1)} %bitcast.103), calls=%async_computation.1 | async-start | bytes 1572864 | tf_op jit(solution)/shard_map/all_to_all | solution.py:179
  141.8 9.8 %all-to-all-done.1 = bf16[16,16,1536]{2,1,0:T(8,128)(2,1)S(1)} async-done(((bf16[16,16,1536]{2,1,0:T(8,128)(2,1)}), bf16[16,16,1536]{2,1,0:T(8,128)(2,1)S(1)}, u32[]{:S(2)}, u32[]{:S(2)}) %all-to-all-start.1) | async-done | bytes 786464 | tf_op jit(solution)/shard_map/all_to_all | solution.py:179
  154.5 23.3 %all_to_all.15 = bf16[16,16,2688]{2,1,0:T(8,128)(2,1)S(1)} all-to-all(bf16[16,16,2688]{2,1,0:T(8,128)(2,1)S(1)} %broadcast_in_dim.95), channel_id=1, replica_groups=mesh['rows_0'=4,'rows_1'=4,'rows_2'=2,'cols'=8] {'rows_0','rows_1'}, dimensions={0} | all-to-all | bytes 2752512 | tf_op jit(solution)/shard_map/all_to_all | solution.py:66
  180.0 2.0 collective-permute-done.23
  186.3 4.3 %collective-permute-start.24 = (f32[8,128]{1,0:T(8,128)S(1)}, f32[8,128]{1,0:T(8,128)S(1)}, u32[]{:S(2)}, u32[]{:S(2)}) collective-permute-start(f32[8,128]{1,0:T(8,128)S(1)} %broadcast_in_dim.96), channel_id=1, source_target_pairs={{0,4},{1,5},{2,6},{3,7},{4,0},{5,1},{6,2},{7,3},{8,12},{9,13},{10,... | collective-permute-start | bytes 12296 | tf_op jit(solution)/shard_map/ppermute | solution.py:24
  200.6 3.2 %collective-permute-start.27 = (bf16[528,128]{1,0:T(8,128)(2,1)S(1)}, bf16[528,128]{1,0:T(8,128)(2,1)S(1)}, u32[]{:S(2)}, u32[]{:S(2)}) collective-permute-start(bf16[528,128]{1,0:T(8,128)(2,1)S(1)} %get-tuple-element.33), channel_id=1, source_target_pairs={{0,7},{1,0},{2,1},{3,2},{4,3},{5,4},{6,5},{7,6},{8,15},{9,8},{10,9... | collective-permute-start | bytes 405512 | tf_op jit(solution)/shard_map/ppermute | solution.py:24
  203.8 4.1 %collective-permute-start.25 = (bf16[528,128]{1,0:T(8,128)(2,1)S(1)}, bf16[528,128]{1,0:T(8,128)(2,1)S(1)}, u32[]{:S(2)}, u32[]{:S(2)}) collective-permute-start(bf16[528,128]{1,0:T(8,128)(2,1)S(1)} %get-tuple-element.31), channel_id=1, source_target_pairs={{0,6},{1,7},{2,0},{3,1},{4,2},{5,3},{6,4},{7,5},{8,14},{9,15},{10,... | collective-permute-start | bytes 405512 | tf_op jit(solution)/shard_map/ppermute | solution.py:24
  209.4 3.1 %collective-permute-done.26 = bf16[528,128]{1,0:T(8,128)(2,1)S(1)} collective-permute-done((bf16[528,128]{1,0:T(8,128)(2,1)S(1)}, bf16[528,128]{1,0:T(8,128)(2,1)S(1)}, u32[]{:S(2)}, u32[]{:S(2)}) %collective-permute-start.26) | collective-permute-done | bytes 135200 | tf_op jit(solution)/shard_map/ppermute | solution.py:24
  222.2 2.4 %fusion.4 = f32[512,128]{1,0:T(8,128)} fusion(f32[512,128]{1,0:T(8,128)S(1)} %copy-done.4, bf16[512,2688]{0,1:T(8,128)(2,1)} %copy-done.1, bf16[512,128]{1,0:T(8,128)(2,1)S(1)} %get-tuple-element.10, bf16[512,128]{1,0:T(8,128)(2,1)S(1)} %get-tuple-element.9, bf16[528,128]{1,0:T(8,128)(2,1)S(1)} %collective-permute-done.28, ...), kind=kOutput, calls=%fused_computation.15 | convolution fusion | flops 135397376 | bytes 2359300 | tf_op jit(solution)/shard_map/dot_general | solution.py:70
  (169 shorter events, 69.2 us)
Async XLA Ops:
  7.2 60.4 %all-gather.3.cloned.1.call-start = ((), (), s32[]{:S(2)}) async-start(), calls=%async_computation.3 | async-start | bytes 4718592 | tf_op jit(solution)/shard_map/all_gather | solution.py:136
  9.2 131.2 %all-gather.5.cloned.1.call-start = ((), (), s32[]{:S(2)}) async-start(), calls=%async_computation.4 | async-start | bytes 1216512 | tf_op jit(solution)/shard_map/all_gather | solution.py:190
  11.8 7.9 %collective-permute-start.9 = (bf16[256,256]{0,1:T(8,128)(2,1)S(1)}, bf16[256,256]{0,1:T(8,128)(2,1)S(1)}, u32[]{:S(2)}, u32[]{:S(2)}) collective-permute-start(bf16[256,256]{0,1:T(8,128)(2,1)S(1)} %maximum_select_fusion.4), channel_id=1, source_target_pairs={{0,64},{64,128},{128,192},{192,0},{1,65},{65,129},{129,193},{193,1... | collective-permute-start | bytes 393224 | tf_op jit(solution)/shard_map/ppermute | solution.py:24
  13.5 8.6 %collective-permute-start.10 = (bf16[256,256]{0,1:T(8,128)(2,1)S(1)}, bf16[256,256]{0,1:T(8,128)(2,1)S(1)}, u32[]{:S(2)}, u32[]{:S(2)}) collective-permute-start(bf16[256,256]{0,1:T(8,128)(2,1)S(1)} %maximum_select_fusion.4), channel_id=1, source_target_pairs={{0,192},{64,0},{128,64},{192,128},{1,193},{65,1},{129,65},{193,129... | collective-permute-start | bytes 393224 | tf_op jit(solution)/shard_map/ppermute | solution.py:24
  17.2 7.8 %collective-permute-start.1 = (bf16[256,256]{0,1:T(8,128)(2,1)S(1)}, bf16[256,256]{0,1:T(8,128)(2,1)S(1)}, u32[]{:S(2)}, u32[]{:S(2)}) collective-permute-start(bf16[256,256]{0,1:T(8,128)(2,1)S(1)} %maximum_select_fusion.2), channel_id=1, source_target_pairs={{0,16},{16,32},{32,48},{48,0},{1,17},{17,33},{33,49},{49,1},{2,18}... | collective-permute-start | bytes 393224 | tf_op jit(solution)/shard_map/ppermute | solution.py:24
  22.9 14.7 %collective-permute-start.12 = (bf16[4,256,256]{2,1,0:T(8,128)(2,1)S(1)}, bf16[4,256,256]{2,1,0:T(8,128)(2,1)}, u32[]{:S(2)}, u32[]{:S(2)}) collective-permute-start(bf16[4,256,256]{2,1,0:T(8,128)(2,1)S(1)} %constant_dynamic-update-slice_fusion), channel_id=1, source_target_pairs={{0,16},{16,32},{32,48},{48,0},{1,17},{17,33},{33,49},{49,1},{2,18}... | collective-permute-start | bytes 1572872 | tf_op jit(solution)/shard_map/ppermute | solution.py:24
  24.4 15.7 %collective-permute-start.13 = (bf16[4,256,256]{2,1,0:T(8,128)(2,1)S(1)}, bf16[4,256,256]{2,1,0:T(8,128)(2,1)}, u32[]{:S(2)}, u32[]{:S(2)}) collective-permute-start(bf16[4,256,256]{2,1,0:T(8,128)(2,1)S(1)} %constant_dynamic-update-slice_fusion), channel_id=1, source_target_pairs={{0,48},{16,0},{32,16},{48,32},{1,49},{17,1},{33,17},{49,33},{2,50}... | collective-permute-start | bytes 1572872 | tf_op jit(solution)/shard_map/ppermute | solution.py:24
  27.3 14.4 %collective-permute-start.4 = (bf16[4,256,256]{2,1,0:T(8,128)(2,1)S(1)}, bf16[4,256,256]{2,1,0:T(8,128)(2,1)}, u32[]{:S(2)}, u32[]{:S(2)}) collective-permute-start(bf16[4,256,256]{2,1,0:T(8,128)(2,1)S(1)} %constant_dynamic-update-slice_fusion.4), channel_id=1, source_target_pairs={{0,64},{64,128},{128,192},{192,0},{1,65},{65,129},{129,193},{193,1... | collective-permute-start | bytes 1572872 | tf_op jit(solution)/shard_map/ppermute | solution.py:24
  27.8 15.7 %collective-permute-start.5 = (bf16[4,256,256]{2,1,0:T(8,128)(2,1)S(1)}, bf16[4,256,256]{2,1,0:T(8,128)(2,1)}, u32[]{:S(2)}, u32[]{:S(2)}) collective-permute-start(bf16[4,256,256]{2,1,0:T(8,128)(2,1)S(1)} %constant_dynamic-update-slice_fusion.4), channel_id=1, source_target_pairs={{0,192},{64,0},{128,64},{192,128},{1,193},{65,1},{129,65},{193,129... | collective-permute-start | bytes 1572872 | tf_op jit(solution)/shard_map/ppermute | solution.py:24
  38.5 14.6 %collective-permute-start.14 = (bf16[2,256,256]{2,1,0:T(8,128)(2,1)S(1)}, bf16[2,256,256]{2,1,0:T(8,128)(2,1)S(1)}, u32[]{:S(2)}, u32[]{:S(2)}) collective-permute-start(bf16[2,256,256]{2,1,0:T(8,128)(2,1)S(1)} %slice.235), channel_id=1, source_target_pairs={{0,16},{16,32},{32,48},{48,0},{1,17},{17,33},{33,49},{49,1},{2,18}... | collective-permute-start | bytes 786440 | tf_op jit(solution)/shard_map/ppermute | solution.py:24
  41.1 12.8 %collective-permute-start.15 = (bf16[2,256,256]{2,1,0:T(8,128)(2,1)S(1)}, bf16[2,256,256]{2,1,0:T(8,128)(2,1)S(1)}, u32[]{:S(2)}, u32[]{:S(2)}) collective-permute-start(bf16[2,256,256]{2,1,0:T(8,128)(2,1)S(1)} %slice.236), channel_id=1, source_target_pairs={{0,48},{16,0},{32,16},{48,32},{1,49},{17,1},{33,17},{49,33},{2,50}... | collective-permute-start | bytes 786440 | tf_op jit(solution)/shard_map/ppermute | solution.py:24
  42.7 12.0 %collective-permute-start.6 = (bf16[2,256,256]{2,1,0:T(8,128)(2,1)S(1)}, bf16[2,256,256]{2,1,0:T(8,128)(2,1)S(1)}, u32[]{:S(2)}, u32[]{:S(2)}) collective-permute-start(bf16[2,256,256]{2,1,0:T(8,128)(2,1)S(1)} %slice.232), channel_id=1, source_target_pairs={{0,64},{64,128},{128,192},{192,0},{1,65},{65,129},{129,193},{193,1... | collective-permute-start | bytes 786440 | tf_op jit(solution)/shard_map/ppermute | solution.py:24
  44.5 10.2 %collective-permute-start.7 = (bf16[2,256,256]{2,1,0:T(8,128)(2,1)S(1)}, bf16[2,256,256]{2,1,0:T(8,128)(2,1)S(1)}, u32[]{:S(2)}, u32[]{:S(2)}) collective-permute-start(bf16[2,256,256]{2,1,0:T(8,128)(2,1)S(1)} %slice.233), channel_id=1, source_target_pairs={{0,192},{64,0},{128,64},{192,128},{1,193},{65,1},{129,65},{193,129... | collective-permute-start | bytes 786440 | tf_op jit(solution)/shard_map/ppermute | solution.py:24
  76.9 13.7 %collective-permute-start.17 = (bf16[512,512]{1,0:T(8,128)(2,1)}, bf16[512,512]{1,0:T(8,128)(2,1)S(1)}, u32[]{:S(2)}, u32[]{:S(2)}) collective-permute-start(bf16[512,512]{1,0:T(8,128)(2,1)} %whitened.1), channel_id=1, source_target_pairs={{0,7},{1,0},{2,1},{3,2},{4,3},{5,4},{6,5},{7,6},{8,15},{9,8},{10,9... | collective-permute-start | bytes 1572872 | tf_op jit(solution)/shard_map/ppermute | solution.py:24
  78.2 16.5 %collective-permute-start.19 = (bf16[512,512]{1,0:T(8,128)(2,1)}, bf16[512,512]{1,0:T(8,128)(2,1)}, u32[]{:S(2)}, u32[]{:S(2)}) collective-permute-start(bf16[512,512]{1,0:T(8,128)(2,1)} %whitened.1), channel_id=1, source_target_pairs={{0,1},{1,2},{2,3},{3,4},{4,5},{5,6},{6,7},{7,0},{8,9},{9,10},{10,1... | collective-permute-start | bytes 1572872 | tf_op jit(solution)/shard_map/ppermute | solution.py:24
  92.0 18.2 %collective-permute-start.21 = (bf16[512,512]{1,0:T(8,128)(2,1)S(1)}, bf16[512,512]{1,0:T(8,128)(2,1)S(1)}, u32[]{:S(2)}, u32[]{:S(2)}) collective-permute-start(bf16[512,512]{1,0:T(8,128)(2,1)S(1)} %collective-permute-done.17), channel_id=1, source_target_pairs={{0,7},{1,0},{2,1},{3,2},{4,3},{5,4},{6,5},{7,6},{8,15},{9,8},{10,9... | collective-permute-start | bytes 1572872 | tf_op jit(solution)/shard_map/ppermute | solution.py:24
  94.7 15.6 %collective-permute-start.20 = (bf16[512,512]{1,0:T(8,128)(2,1)}, bf16[512,512]{1,0:T(8,128)(2,1)}, u32[]{:S(2)}, u32[]{:S(2)}) collective-permute-start(bf16[512,512]{1,0:T(8,128)(2,1)} %collective-permute-done.19), channel_id=1, source_target_pairs={{0,1},{1,2},{2,3},{3,4},{4,5},{5,6},{6,7},{7,0},{8,9},{9,10},{10,1... | collective-permute-start | bytes 1572872 | tf_op jit(solution)/shard_map/ppermute | solution.py:24
  114.5 8.0 %collective-permute-start.22 = (bf16[256,1536]{1,0:T(8,128)(2,1)}, bf16[256,1536]{1,0:T(8,128)(2,1)}, u32[]{:S(2)}, u32[]{:S(2)}) collective-permute-start(bf16[256,1536]{1,0:T(8,128)(2,1)} %dynamic-slice_convert_fusion), channel_id=1, source_target_pairs={{0,8},{8,0},{1,9},{9,1},{2,10},{10,2},{3,11},{11,3},{4,12},{12,4},... | collective-permute-start | bytes 2359304 | tf_op jit(solution)/shard_map/ppermute | solution.py:24
  114.5 19.3 %all-to-all-start = ((bf16[16,16,1024]{2,1,0:T(8,128)(2,1)}), bf16[16,16,1024]{2,1,0:T(8,128)(2,1)}, u32[]{:S(2)}, u32[]{:S(2)}) async-start(bf16[16,16,1024]{2,1,0:T(8,128)(2,1)} %bitcast.104), calls=%async_computation | async-start | bytes 1048576 | tf_op jit(solution)/shard_map/all_to_all | solution.py:179
  133.8 17.7 %all-to-all-start.1 = ((bf16[16,16,1536]{2,1,0:T(8,128)(2,1)}), bf16[16,16,1536]{2,1,0:T(8,128)(2,1)S(1)}, u32[]{:S(2)}, u32[]{:S(2)}) async-start(bf16[16,16,1536]{2,1,0:T(8,128)(2,1)} %bitcast.103), calls=%async_computation.1 | async-start | bytes 1572864 | tf_op jit(solution)/shard_map/all_to_all | solution.py:179
  199.9 8.0 %collective-permute-start.28 = (bf16[528,128]{1,0:T(8,128)(2,1)S(1)}, bf16[528,128]{1,0:T(8,128)(2,1)S(1)}, u32[]{:S(2)}, u32[]{:S(2)}) collective-permute-start(bf16[528,128]{1,0:T(8,128)(2,1)S(1)} %get-tuple-element.34), channel_id=1, source_target_pairs={{0,1},{1,2},{2,3},{3,4},{4,5},{5,6},{6,7},{7,0},{8,9},{9,10},{10,1... | collective-permute-start | bytes 405512 | tf_op jit(solution)/shard_map/ppermute | solution.py:24
  200.6 8.1 %collective-permute-start.27 = (bf16[528,128]{1,0:T(8,128)(2,1)S(1)}, bf16[528,128]{1,0:T(8,128)(2,1)S(1)}, u32[]{:S(2)}, u32[]{:S(2)}) collective-permute-start(bf16[528,128]{1,0:T(8,128)(2,1)S(1)} %get-tuple-element.33), channel_id=1, source_target_pairs={{0,7},{1,0},{2,1},{3,2},{4,3},{5,4},{6,5},{7,6},{8,15},{9,8},{10,9... | collective-permute-start | bytes 405512 | tf_op jit(solution)/shard_map/ppermute | solution.py:24
  203.8 8.8 %collective-permute-start.26 = (bf16[528,128]{1,0:T(8,128)(2,1)S(1)}, bf16[528,128]{1,0:T(8,128)(2,1)S(1)}, u32[]{:S(2)}, u32[]{:S(2)}) collective-permute-start(bf16[528,128]{1,0:T(8,128)(2,1)S(1)} %get-tuple-element.32), channel_id=1, source_target_pairs={{0,2},{1,3},{2,4},{3,5},{4,6},{5,7},{6,0},{7,1},{8,10},{9,11},{10,... | collective-permute-start | bytes 405512 | tf_op jit(solution)/shard_map/ppermute | solution.py:24
  203.8 9.6 %collective-permute-start.25 = (bf16[528,128]{1,0:T(8,128)(2,1)S(1)}, bf16[528,128]{1,0:T(8,128)(2,1)S(1)}, u32[]{:S(2)}, u32[]{:S(2)}) collective-permute-start(bf16[528,128]{1,0:T(8,128)(2,1)S(1)} %get-tuple-element.31), channel_id=1, source_target_pairs={{0,6},{1,7},{2,0},{3,1},{4,2},{5,3},{6,4},{7,5},{8,14},{9,15},{10,... | collective-permute-start | bytes 405512 | tf_op jit(solution)/shard_map/ppermute | solution.py:24
  (16 other events, 122.5 us)
Sparse Core Ops, SparseCore 0:
  9.8 57.7 all-gather.2
  95.5 39.0 all-gather.4

commit v2 on v1

--- a/solution.py
+++ b/solution.py
@@ -72,15 +72,9 @@
     )
 
 
-def split(value):
-    high = lax.reduce_precision(value, 8, 7)
-    middle = lax.reduce_precision(value - high, 8, 7)
-    return [t.astype(bf16) for t in (high, middle, value - high - middle)]
-
-
-def whitened_kernel(core_ref, scale_ref, both_ref, q_ref, q_other_ref, inv_ref, inv_other_ref, out_ref, sums):
+def whitened_kernel(core_ref, scale_ref, more_ref, both_ref, q_ref, q_other_ref, inv_ref, inv_other_ref, out_ref, sums):
     step = pl.program_id(0)
-    rows, columns = out_ref.shape[0] // 2, out_ref.shape[1] // 2
+    rows, columns = both_ref.shape[0] // 2, out_ref.shape[1] // 2
 
     @pl.when(step == 0)
     def _():
@@ -97,34 +91,35 @@
     def _():
         mine, others = (scale_ref[...] * sums[j] for j in range(2))
         first = core_ref[0] == 0
-        out_ref[:, :columns] = jnp.where(first, mine, others).astype(out_ref.dtype)
-        out_ref[:, columns:] = jnp.where(first, others, mine).astype(out_ref.dtype)
-
-
-def whitened(core, scale, both, *factors):
+        out_ref[: 2 * rows, :columns] = jnp.where(first, mine, others).astype(out_ref.dtype)
+        out_ref[: 2 * rows, columns:] = jnp.where(first, others, mine).astype(out_ref.dtype)
+        out_ref[2 * rows :, :] = more_ref[...]
+
+
+def whitened(core, scale, more, both, *factors):
     (rows, depth), half = both.shape, factors[0].shape[1]
     deep = min(512, depth)
     return pl.pallas_call(
         whitened_kernel,
         grid=(depth // deep,),
-        out_shape=jax.ShapeDtypeStruct((rows, 2 * half), bf16),
+        out_shape=jax.ShapeDtypeStruct((rows + more.shape[0], 2 * half), bf16),
         in_specs=[
             pl.BlockSpec(memory_space=pltpu.SMEM),
             pl.BlockSpec((rows, 1), lambda k: (0, 0)),
+            pl.BlockSpec(more.shape, lambda k: (0, 0)),
             pl.BlockSpec((rows, deep), lambda k: (0, k)),
             *[pl.BlockSpec((deep, half), lambda k: (k, 0)) for _ in factors],
         ],
-        out_specs=pl.BlockSpec((rows, 2 * half), lambda k: (0, 0)),
+        out_specs=pl.BlockSpec((rows + more.shape[0], 2 * half), lambda k: (0, 0)),
         scratch_shapes=[pltpu.VMEM((2, rows, half), f32)],
         cost_estimate=pl.CostEstimate(
             flops=4 * rows * depth * half, bytes_accessed=2 * depth * (rows + 4 * half), transcendentals=0
         ),
         name="whitened",
-    )(core[None], scale, both, *factors)
+    )(core[None], scale, more, both, *factors)
 
 
 def body(grads, probe, left_factor, q_right, q_inv_t):
-    n_cols, me = lax.axis_size(COLS), lax.axis_index(COLS)
     core = lax.axis_index(CORE)
     n_plane = lax.axis_size(PLANE)
     height, width = grads.shape
@@ -152,8 +147,8 @@
     q_other, inv_other = shift(q_half, CORE, 1), shift(inv_half, CORE, 1)
 
     scale = jnp.concatenate([left_factor, 1.0 / left_factor])[:, None]
-    own = whitened(core, scale, both, q_half, q_other, inv_half, inv_other)
-    white, conj = own[:height], own[height:]
+    own = whitened(core, scale, q_t, both, q_half, q_other, inv_half, inv_other)
+    white, conj = own[:height], own[height : 2 * height]
 
     before = shift(own, COLS, 1)
     behind = shift(own, COLS, -1)
@@ -161,8 +156,8 @@
     behind_2 = shift(behind, COLS, -1)
 
     def pair(left, right):
-        signed = jnp.concatenate([right[:height], -right[height:]], axis=0)
-        return with_layout_constraint(dot(left, signed, 0, 0), Layout(major_to_minor=(0, 1)))
+        signed = jnp.concatenate([right[:height], -right[height : 2 * height]], axis=0)
+        return with_layout_constraint(dot(left[: 2 * height], signed, 0, 0), Layout(major_to_minor=(0, 1)))
 
     def over_cores(pairs):
         products = []
@@ -183,14 +178,8 @@
     early = over_plane(early_part)
     white_f, conj_f = white.astype(f32), conj.astype(f32)
     left_part = jnp.sum(white_f * white_f - conj_f * conj_f, axis=1)
-    strip = q_low.shape[1]
-    lines = height // strip
-    terms = jnp.stack(split(left_part)).reshape(3 * lines, strip)
-    terms = jnp.pad(terms, ((0, 16 - 3 * lines), (0, 0)))
-    q_all = lax.all_gather(jnp.concatenate([q_low, terms], axis=0), COLS, axis=0, tiled=True)
-    q_all = q_all.reshape(n_cols, width + 16, -1)
-    terms = q_all[:, width : width + 3 * lines].astype(f32).reshape(n_cols, 3, height)
-    left_grad = jnp.sum((terms[:, 0] + terms[:, 1]) + terms[:, 2], axis=0)
+    left_parts = from_everyone(left_part.reshape(-1, 128), COLS)
+    left_grad = jnp.sum(left_parts, axis=0).reshape(height)
     top_l = jnp.max(jnp.abs(left_grad))
     before_2, behind_2, _ = lax.optimization_barrier((before_2, behind_2, early_part))
     late_part = over_cores([(before, behind), (before, behind_2), (before_2, behind_2)])
@@ -198,47 +187,38 @@
 
 
     top_r = jnp.maximum(jnp.max(jnp.abs(early)), jnp.max(jnp.abs(late)))
-    terms = jnp.stack(split(jnp.stack([top_r, top_l]))).reshape(1, 6)
-    note = jnp.broadcast_to(jnp.pad(terms, ((0, 0), (0, 122))), (piece, 128))
-    pieces = jnp.concatenate([early.astype(bf16), late.astype(bf16), note], axis=1)
+    line = lax.broadcasted_iota(jnp.int32, (8, 128), 0)
+    tops = lax.optimization_barrier(jnp.where(line == 0, top_r, top_l))
+    tops = lax.all_gather(tops, (*ROWS, COLS), axis=0)
+    tops = jnp.max(tops, axis=0)
+    scale_r, scale_l = (learn_rate / (tops[i, 0] + epsilon) for i in range(2))
+
+    pieces = jnp.concatenate([early.astype(bf16), late.astype(bf16)], axis=1)
     mine = from_everyone(pieces, PLANE).reshape(half, -1)
     gram = in_core_order(mine, shift(mine, CORE, 1), 0)
 
-    def joined(terms):
-        terms = terms.astype(f32)
-        return (terms[:, 0] + terms[:, 1]) + terms[:, 2]
-
-    top_r, top_l = jnp.max(joined(gram[:, 5 * width : 5 * width + 6].reshape(width, 3, 2)), axis=0)
-    top_r = jnp.full((8, 128), top_r)
-    top_r = jnp.maximum(top_r, shift(top_r, COLS, n_cols // 2))[0, 0]
-
     def block(i, size=1):
         return gram[:, i * width : (i + size) * width]
 
-    def q_at(by, size=1):
-        rows = [
-            lax.dynamic_index_in_dim(q_all, (me + by + i + n_cols) % n_cols, 0, keepdims=False)[:width]
-            for i in range(size)
-        ]
-        return jnp.concatenate(rows, axis=0)
-
-    note = jnp.pad(jnp.stack(split(top_r))[:, None], ((0, 13), (0, strip - 1)))
+    q_near = {i: v[2 * height :] for i, v in ((-1, before), (0, own), (1, behind), (2, behind_2))}
+
+    def times(i, by):
+        value, q = block(i, len(by)), jnp.concatenate([q_near[j] for j in by], axis=1)
+        return dot(value, q, 1, 1)
+
+    def turned_times(i, by):
+        return dot(block(i), q_near[by], 0, 1)
 
     def sent(value, by):
-        return shift(jnp.concatenate([value.astype(bf16), note], axis=0), COLS, by)
+        return shift(value.astype(bf16), COLS, by).astype(f32)
 
     got = [
-        sent(dot(block(4), q_at(2), 1, 0), -2),
-        sent(dot(block(3), q_at(-1), 0, 0), 2),
-        sent(dot(block(2, 2), q_at(1, 2), 1, 0), -1),
-        sent(dot(block(1), q_at(0), 0, 0) + dot(block(2), q_at(-1), 0, 0), 1),
+        sent(times(4, (2,)), -2),
+        sent(turned_times(3, -1), 2),
+        sent(times(2, (1, 2)), -1),
+        sent(turned_times(1, 0) + turned_times(2, -1), 1),
     ]
-    product = dot(block(0, 2), q_at(0, 2), 1, 0)
-    for value in got:
-        product = product + value[:width].astype(f32)
-        top_r = jnp.maximum(top_r, joined(value[width : width + 3, :1].T)[0])
-    scale_r = learn_rate / (top_r + epsilon)
-    scale_l = learn_rate / (top_l + epsilon)
+    product = times(0, (0, 1)) + ((got[0] + got[1]) + (got[2] + got[3]))
     left_new = left_factor - scale_l * left_grad * left_factor
     q_new = q_right - scale_r * product
     return (left_new, q_new)

time: 234 us -> 310 us (1.32)
  waiting for transfers between devices: 62.6 us -> 176 us
  between operations: 29.3 us -> 17.2 us
  blocking collectives: 23.3 us -> 11.8 us
  other arithmetic: 18.5 us -> 13.3 us
  matrix products: 13.9 us -> 9.02 us
    all_gather x1, waiting for transfers between devices: 0.01 us -> 85.6 us  [body(): tops = lax.all_gather(tops, (*ROWS, COLS), axis=0)]
    ppermute x29 -> x28, waiting for transfers between devices: 38.3 us -> 56.7 us  [shift(): lax.ppermute(value, axis, [(i, (i + by) % size) for i in range(size)])]
    all_to_all x0 -> x1, waiting for transfers between devices: none -> 14 us  [from_everyone(): return lax.all_to_all(copies, axes, 0, 0, tiled=True)]
    all_to_all x1, blocking collectives: 23.3 us -> 11.8 us  [from_everyone(): return lax.all_to_all(copies, axes, 0, 0, tiled=True)]
    ppermute x29 -> x28, starting transfers between devices: 38.1 us -> 30.8 us  [shift(): lax.ppermute(value, axis, [(i, (i + by) % size) for i in range(size)])]
    all_to_all x0 -> x1, starting transfers between devices: none -> 4.95 us  [from_everyone(): return lax.all_to_all(copies, axes, 0, 0, tiled=True)]
    dot_general x11, matrix products: 13.9 us -> 9.02 us  [dot(): lax.dot_general(left, right, (((left_dim,), (right_dim,)), ((), ())), pre...]
    dynamic_update_slice x5, local copies, waits for them, and re-layouts: 2.24 us -> 6.11 us  [put_plane(): return lax.dynamic_update_slice(plane, block[None], (owner, begin, 0, 0))]
  transfers between devices with their start and end apart: 33 -> 33, of which waited for: 13 -> 17; matrix products, arithmetic and copies ran while one was open for 18% -> 11% of each run, Pallas kernels for 0% -> 0%
where the time goes in v2:
time: 310 us; the launch traced here: 309 us
  waiting for transfers between devices  176 us (57%)
  starting transfers between devices  50.2 us (16%)
  local copies, waits for them, and re-layouts  22.2 us (7%)
  between operations  17.2 us (6%)
  other arithmetic  13.3 us (4%)
  blocking collectives  11.8 us (4%)
  Pallas kernels  9.44 us (3%)
  matrix products  9.02 us (3%)
    all_gather x1, waiting for transfers between devices, body(): tops = lax.all_gather(tops, (*ROWS, COLS), axis=0)  85.6 us
    ppermute x28, waiting for transfers between devices, shift(): lax.ppermute(value, axis, [(i, (i + by) % size) for i in range(size)])  56.7 us
    ppermute x28, starting transfers between devices, shift(): lax.ppermute(value, axis, [(i, (i + by) % size) for i in range(size)])  30.8 us
    all_to_all x2, waiting for transfers between devices, over_plane(): parts = lax.all_to_all(part, PLANE, 0, 0, tiled=True)  17.3 us
    all_to_all x2, starting transfers between devices, over_plane(): parts = lax.all_to_all(part, PLANE, 0, 0, tiled=True)  14.4 us
    all_to_all x1, waiting for transfers between devices, from_everyone(): return lax.all_to_all(copies, axes, 0, 0, tiled=True)  14 us
    all_to_all x1, blocking collectives, from_everyone(): return lax.all_to_all(copies, axes, 0, 0, tiled=True)  11.8 us
    pallas_call x1, Pallas kernels, whitened(): pl.pallas_call(whitened_kernel, grid=(depth // deep,), out_shape=jax.Shap...  9.44 us
  transfers between devices with their start and end apart: 33, of which 17 were waited for; matrix products, arithmetic and copies ran while one was open for 11% of the time, Pallas kernels for 0%

profile of v2, /device:TPU:2, one launch (start us, length us, event | category | flops | bytes accessed | tf_op | source)
XLA Modules:
  0.0 309.1 jit_solution(11934824069297502978)
XLA Ops:
  11.9 2.2 collective-permute-start.3
  16.2 3.3 %collective-permute-start.11 = (bf16[256,256]{1,0:T(8,128)(2,1)S(1)}, bf16[256,256]{1,0:T(8,128)(2,1)S(1)}, u32[]{:S(2)}, u32[]{:S(2)}) collective-permute-start(bf16[256,256]{1,0:T(8,128)(2,1)S(1)} %maximum_select_fusion.4), channel_id=1, source_target_pairs={{0,128},{64,192},{128,0},{192,64},{1,129},{65,193},{129,1},{193,65... | collective-permute-start | bytes 393224 | tf_op jit(solution)/shard_map/ppermute | solution.py:24
  20.3 5.6 %collective-permute-done.9 = bf16[256,256]{1,0:T(8,128)(2,1)S(1)} collective-permute-done((bf16[256,256]{1,0:T(8,128)(2,1)S(1)}, bf16[256,256]{1,0:T(8,128)(2,1)S(1)}, u32[]{:S(2)}, u32[]{:S(2)}) %collective-permute-start.9) | collective-permute-done | bytes 131104 | tf_op jit(solution)/shard_map/ppermute | solution.py:24
  26.2 4.7 %collective-permute-done.10 = bf16[256,256]{1,0:T(8,128)(2,1)S(1)} collective-permute-done((bf16[256,256]{1,0:T(8,128)(2,1)S(1)}, bf16[256,256]{1,0:T(8,128)(2,1)S(1)}, u32[]{:S(2)}, u32[]{:S(2)}) %collective-permute-start.10) | collective-permute-done | bytes 131104 | tf_op jit(solution)/shard_map/ppermute | solution.py:24
  37.9 5.3 %collective-permute-done.13 = bf16[4,256,256]{2,1,0:T(8,128)(2,1)} collective-permute-done((bf16[4,256,256]{2,1,0:T(8,128)(2,1)S(1)}, bf16[4,256,256]{2,1,0:T(8,128)(2,1)}, u32[]{:S(2)}, u32[]{:S(2)}) %collective-permute-start.13) | collective-permute-done | bytes 524320 | tf_op jit(solution)/shard_map/ppermute | solution.py:24
  62.0 3.0 collective-permute-done.8.q_other_ref
  65.0 2.5 all-gather.4.cloned.1.call-done.both_ref
  67.5 9.4 %whitened.1 = bf16[640,512]{1,0:T(8,128)(2,1)} custom-call(s32[1]{0:T(128)} %bitcast.core_ref, f32[512,1]{1,0:T(8,128)} %copy.33.scale_ref, bf16[128,512]{1,0:T(8,128)(2,1)} %bitcast.79, bf16[512,4096]{1,0:T(8,128)(2,1)} %all-gather.4.cloned.1.call-done.both_ref, bf16[4096,256]{1,0:T(8,128)(2,1)} %bitcast.17.q_ref, ...), custom_call_target="tpu_custom_call" | custom-call | flops 2147483648 | bytes 12582912 | tf_op jit(solution)/shard_map/whitened/pallas_call | solution.py:102
  77.0 3.5 %collective-permute-start.17 = (bf16[640,512]{1,0:T(8,128)(2,1)}, bf16[640,512]{1,0:T(8,128)(2,1)S(1)}, u32[]{:S(2)}, u32[]{:S(2)}) collective-permute-start(bf16[640,512]{1,0:T(8,128)(2,1)} %whitened.1), channel_id=1, source_target_pairs={{0,7},{1,0},{2,1},{3,2},{4,3},{5,4},{6,5},{7,6},{8,15},{9,8},{10,9... | collective-permute-start | bytes 1966088 | tf_op jit(solution)/shard_map/ppermute | solution.py:24
  83.1 12.0 %collective-permute-done.17 = bf16[640,512]{1,0:T(8,128)(2,1)S(1)} collective-permute-done((bf16[640,512]{1,0:T(8,128)(2,1)}, bf16[640,512]{1,0:T(8,128)(2,1)S(1)}, u32[]{:S(2)}, u32[]{:S(2)}) %collective-permute-start.17) | collective-permute-done | bytes 655392 | tf_op jit(solution)/shard_map/ppermute | solution.py:24
  95.8 2.6 collective-permute-done.19
  98.4 3.2 %collective-permute-start.21 = (bf16[640,512]{1,0:T(8,128)(2,1)S(1)}, bf16[640,512]{1,0:T(8,128)(2,1)S(1)}, u32[]{:S(2)}, u32[]{:S(2)}) collective-permute-start(bf16[640,512]{1,0:T(8,128)(2,1)S(1)} %collective-permute-done.17), channel_id=1, source_target_pairs={{0,7},{1,0},{2,1},{3,2},{4,3},{5,4},{6,5},{7,6},{8,15},{9,8},{10,9... | collective-permute-start | bytes 1966088 | tf_op jit(solution)/shard_map/ppermute | solution.py:24
  103.0 12.2 %collective-permute-done.20 = bf16[640,512]{1,0:T(8,128)(2,1)S(1)} collective-permute-done((bf16[640,512]{1,0:T(8,128)(2,1)S(1)}, bf16[640,512]{1,0:T(8,128)(2,1)S(1)}, u32[]{:S(2)}, u32[]{:S(2)}) %collective-permute-start.20) | collective-permute-done | bytes 655392 | tf_op jit(solution)/shard_map/ppermute | solution.py:24
  117.9 11.8 %all_to_all.20 = f32[8,2,128]{2,1,0:T(2,128)S(1)} all-to-all(f32[8,2,128]{2,1,0:T(2,128)S(1)} %broadcast_in_dim.97), channel_id=1, replica_groups=mesh['rows_0'=4,'rows_1'=4,'rows_2'=2,'cols'=8] {'cols'}, dimensions={0} | all-to-all | bytes 16384 | tf_op jit(solution)/shard_map/all_to_all | solution.py:66
  129.7 9.6 %all-to-all-start = ((bf16[16,16,1024]{2,1,0:T(8,128)(2,1)}), bf16[16,16,1024]{2,1,0:T(8,128)(2,1)}, u32[]{:S(2)}, u32[]{:S(2)}) async-start(bf16[16,16,1024]{2,1,0:T(8,128)(2,1)} %bitcast.78), calls=%async_computation | async-start | bytes 1048576 | tf_op jit(solution)/shard_map/all_to_all | solution.py:174
  139.2 2.2 add_convert_fusion
  141.4 7.3 %all-to-all-done = bf16[16,16,1024]{2,1,0:T(8,128)(2,1)} async-done(((bf16[16,16,1024]{2,1,0:T(8,128)(2,1)}), bf16[16,16,1024]{2,1,0:T(8,128)(2,1)}, u32[]{:S(2)}, u32[]{:S(2)}) %all-to-all-start) | async-done | bytes 524320 | tf_op jit(solution)/shard_map/all_to_all | solution.py:174
  148.8 4.8 %all-to-all-start.1 = ((bf16[16,16,1536]{2,1,0:T(8,128)(2,1)}), bf16[16,16,1536]{2,1,0:T(8,128)(2,1)S(1)}, u32[]{:S(2)}, u32[]{:S(2)}) async-start(bf16[16,16,1536]{2,1,0:T(8,128)(2,1)} %bitcast.77), calls=%async_computation.1 | async-start | bytes 1572864 | tf_op jit(solution)/shard_map/all_to_all | solution.py:174
  155.4 9.9 %all-to-all-done.1 = bf16[16,16,1536]{2,1,0:T(8,128)(2,1)S(1)} async-done(((bf16[16,16,1536]{2,1,0:T(8,128)(2,1)}), bf16[16,16,1536]{2,1,0:T(8,128)(2,1)S(1)}, u32[]{:S(2)}, u32[]{:S(2)}) %all-to-all-start.1) | async-done | bytes 786464 | tf_op jit(solution)/shard_map/all_to_all | solution.py:174
  167.2 5.0 %all-to-all-start.3 = ((bf16[16,16,2560]{2,1,0:T(8,128)(2,1)}), bf16[16,16,2560]{2,1,0:T(8,128)(2,1)S(1)}, u32[]{:S(2)}, u32[]{:S(2)}) async-start(bf16[16,16,2560]{2,1,0:T(8,128)(2,1)} %broadcast_in_dim.99), calls=%async_computation.3 | async-start | bytes 2621440 | tf_op jit(solution)/shard_map/all_to_all | solution.py:66
  175.3 14.0 %all-to-all-done.3 = bf16[16,16,2560]{2,1,0:T(8,128)(2,1)S(1)} async-done(((bf16[16,16,2560]{2,1,0:T(8,128)(2,1)}), bf16[16,16,2560]{2,1,0:T(8,128)(2,1)S(1)}, u32[]{:S(2)}, u32[]{:S(2)}) %all-to-all-start.3) | async-done | bytes 1310752 | tf_op jit(solution)/shard_map/all_to_all | solution.py:66
  191.2 85.6 %all-gather.6.cloned.1.call-done = f32[2048,128]{1,0:T(8,128)} async-done(((f32[8,128]{1,0:T(8,128)}), f32[2048,128]{1,0:T(8,128)}) %all-gather.6.cloned.1.call-update) | async-done | bytes 1048592 | tf_op jit(solution)/shard_map/all_gather | solution.py:192
  292.9 4.8 %collective-permute-done.25 = bf16[512,128]{1,0:T(8,128)(2,1)S(1)} collective-permute-done((bf16[512,128]{1,0:T(8,128)(2,1)S(1)}, bf16[512,128]{1,0:T(8,128)(2,1)S(1)}, u32[]{:S(2)}, u32[]{:S(2)}) %collective-permute-start.25) | collective-permute-done | bytes 131104 | tf_op jit(solution)/shard_map/ppermute | solution.py:24
  297.7 3.3 %collective-permute-done.24 = bf16[512,128]{1,0:T(8,128)(2,1)S(1)} collective-permute-done((bf16[512,128]{1,0:T(8,128)(2,1)S(1)}, bf16[512,128]{1,0:T(8,128)(2,1)S(1)}, u32[]{:S(2)}, u32[]{:S(2)}) %collective-permute-start.24) | collective-permute-done | bytes 131104 | tf_op jit(solution)/shard_map/ppermute | solution.py:24
  (142 shorter events, 64.1 us)
Async XLA Ops:
  7.2 60.3 %all-gather.4.cloned.1.call-start = ((), (), s32[]{:S(2)}) async-start(), calls=%async_computation.4 | async-start | bytes 4718592 | tf_op jit(solution)/shard_map/all_gather | solution.py:131
  11.9 21.2 %collective-permute-start.3 = (bf16[256,256]{1,0:T(8,128)(2,1)S(1)}, bf16[256,256]{1,0:T(8,128)(2,1)S(1)}, u32[]{:S(2)}, u32[]{:S(2)}) collective-permute-start(bf16[256,256]{1,0:T(8,128)(2,1)S(1)} %maximum_select_fusion.2), channel_id=1, source_target_pairs={{0,32},{16,48},{32,0},{48,16},{1,33},{17,49},{33,1},{49,17},{2,34}... | collective-permute-start | bytes 393224 | tf_op jit(solution)/shard_map/ppermute | solution.py:24
  14.1 18.9 %collective-permute-start.2 = (bf16[256,256]{1,0:T(8,128)(2,1)S(1)}, bf16[256,256]{1,0:T(8,128)(2,1)S(1)}, u32[]{:S(2)}, u32[]{:S(2)}) collective-permute-start(bf16[256,256]{1,0:T(8,128)(2,1)S(1)} %maximum_select_fusion.2), channel_id=1, source_target_pairs={{0,48},{16,0},{32,16},{48,32},{1,49},{17,1},{33,17},{49,33},{2,50}... | collective-permute-start | bytes 393224 | tf_op jit(solution)/shard_map/ppermute | solution.py:24
  15.6 17.5 %collective-permute-start.1 = (bf16[256,256]{1,0:T(8,128)(2,1)S(1)}, bf16[256,256]{1,0:T(8,128)(2,1)S(1)}, u32[]{:S(2)}, u32[]{:S(2)}) collective-permute-start(bf16[256,256]{1,0:T(8,128)(2,1)S(1)} %maximum_select_fusion.2), channel_id=1, source_target_pairs={{0,16},{16,32},{32,48},{48,0},{1,17},{17,33},{33,49},{49,1},{2,18}... | collective-permute-start | bytes 393224 | tf_op jit(solution)/shard_map/ppermute | solution.py:24
  16.2 14.7 %collective-permute-start.11 = (bf16[256,256]{1,0:T(8,128)(2,1)S(1)}, bf16[256,256]{1,0:T(8,128)(2,1)S(1)}, u32[]{:S(2)}, u32[]{:S(2)}) collective-permute-start(bf16[256,256]{1,0:T(8,128)(2,1)S(1)} %maximum_select_fusion.4), channel_id=1, source_target_pairs={{0,128},{64,192},{128,0},{192,64},{1,129},{65,193},{129,1},{193,65... | collective-permute-start | bytes 393224 | tf_op jit(solution)/shard_map/ppermute | solution.py:24
  30.9 12.2 %collective-permute-start.13 = (bf16[4,256,256]{2,1,0:T(8,128)(2,1)S(1)}, bf16[4,256,256]{2,1,0:T(8,128)(2,1)}, u32[]{:S(2)}, u32[]{:S(2)}) collective-permute-start(bf16[4,256,256]{2,1,0:T(8,128)(2,1)S(1)} %bitcast_dynamic-update-slice_fusion.10), channel_id=1, source_target_pairs={{0,48},{16,0},{32,16},{48,32},{1,49},{17,1},{33,17},{49,33},{2,50}... | collective-permute-start | bytes 1572872 | tf_op jit(solution)/shard_map/ppermute | solution.py:24
  32.5 13.2 %collective-permute-start.12 = (bf16[4,256,256]{2,1,0:T(8,128)(2,1)S(1)}, bf16[4,256,256]{2,1,0:T(8,128)(2,1)}, u32[]{:S(2)}, u32[]{:S(2)}) collective-permute-start(bf16[4,256,256]{2,1,0:T(8,128)(2,1)S(1)} %bitcast_dynamic-update-slice_fusion.10), channel_id=1, source_target_pairs={{0,16},{16,32},{32,48},{48,0},{1,17},{17,33},{33,49},{49,1},{2,18}... | collective-permute-start | bytes 1572872 | tf_op jit(solution)/shard_map/ppermute | solution.py:24
  33.1 14.2 %collective-permute-start.5 = (bf16[4,256,256]{2,1,0:T(8,128)(2,1)S(1)}, bf16[4,256,256]{2,1,0:T(8,128)(2,1)}, u32[]{:S(2)}, u32[]{:S(2)}) collective-permute-start(bf16[4,256,256]{2,1,0:T(8,128)(2,1)S(1)} %bitcast_dynamic-update-slice_fusion.13), channel_id=1, source_target_pairs={{0,192},{64,0},{128,64},{192,128},{1,193},{65,1},{129,65},{193,129... | collective-permute-start | bytes 1572872 | tf_op jit(solution)/shard_map/ppermute | solution.py:24
  34.6 14.8 %collective-permute-start.4 = (bf16[4,256,256]{2,1,0:T(8,128)(2,1)S(1)}, bf16[4,256,256]{2,1,0:T(8,128)(2,1)}, u32[]{:S(2)}, u32[]{:S(2)}) collective-permute-start(bf16[4,256,256]{2,1,0:T(8,128)(2,1)S(1)} %bitcast_dynamic-update-slice_fusion.13), channel_id=1, source_target_pairs={{0,64},{64,128},{128,192},{192,0},{1,65},{65,129},{129,193},{193,1... | collective-permute-start | bytes 1572872 | tf_op jit(solution)/shard_map/ppermute | solution.py:24
  44.2 13.4 %collective-permute-start.15 = (bf16[2,256,256]{2,1,0:T(8,128)(2,1)S(1)}, bf16[2,256,256]{2,1,0:T(8,128)(2,1)S(1)}, u32[]{:S(2)}, u32[]{:S(2)}) collective-permute-start(bf16[2,256,256]{2,1,0:T(8,128)(2,1)S(1)} %slice.121), channel_id=1, source_target_pairs={{0,48},{16,0},{32,16},{48,32},{1,49},{17,1},{33,17},{49,33},{2,50}... | collective-permute-start | bytes 786440 | tf_op jit(solution)/shard_map/ppermute | solution.py:24
  46.6 10.9 %collective-permute-start.14 = (bf16[2,256,256]{2,1,0:T(8,128)(2,1)S(1)}, bf16[2,256,256]{2,1,0:T(8,128)(2,1)S(1)}, u32[]{:S(2)}, u32[]{:S(2)}) collective-permute-start(bf16[2,256,256]{2,1,0:T(8,128)(2,1)S(1)} %slice.120), channel_id=1, source_target_pairs={{0,16},{16,32},{32,48},{48,0},{1,17},{17,33},{33,49},{49,1},{2,18}... | collective-permute-start | bytes 786440 | tf_op jit(solution)/shard_map/ppermute | solution.py:24
  48.3 10.8 %collective-permute-start.7 = (bf16[2,256,256]{2,1,0:T(8,128)(2,1)S(1)}, bf16[2,256,256]{2,1,0:T(8,128)(2,1)S(1)}, u32[]{:S(2)}, u32[]{:S(2)}) collective-permute-start(bf16[2,256,256]{2,1,0:T(8,128)(2,1)S(1)} %slice.118), channel_id=1, source_target_pairs={{0,192},{64,0},{128,64},{192,128},{1,193},{65,1},{129,65},{193,129... | collective-permute-start | bytes 786440 | tf_op jit(solution)/shard_map/ppermute | solution.py:24
  77.0 18.1 %collective-permute-start.17 = (bf16[640,512]{1,0:T(8,128)(2,1)}, bf16[640,512]{1,0:T(8,128)(2,1)S(1)}, u32[]{:S(2)}, u32[]{:S(2)}) collective-permute-start(bf16[640,512]{1,0:T(8,128)(2,1)} %whitened.1), channel_id=1, source_target_pairs={{0,7},{1,0},{2,1},{3,2},{4,3},{5,4},{6,5},{7,6},{8,15},{9,8},{10,9... | collective-permute-start | bytes 1966088 | tf_op jit(solution)/shard_map/ppermute | solution.py:24
  80.5 17.9 %collective-permute-start.19 = (bf16[640,512]{1,0:T(8,128)(2,1)}, bf16[640,512]{1,0:T(8,128)(2,1)S(1)}, u32[]{:S(2)}, u32[]{:S(2)}) collective-permute-start(bf16[640,512]{1,0:T(8,128)(2,1)} %whitened.1), channel_id=1, source_target_pairs={{0,1},{1,2},{2,3},{3,4},{4,5},{5,6},{6,7},{7,0},{8,9},{9,10},{10,1... | collective-permute-start | bytes 1966088 | tf_op jit(solution)/shard_map/ppermute | solution.py:24
  98.4 16.8 %collective-permute-start.20 = (bf16[640,512]{1,0:T(8,128)(2,1)S(1)}, bf16[640,512]{1,0:T(8,128)(2,1)S(1)}, u32[]{:S(2)}, u32[]{:S(2)}) collective-permute-start(bf16[640,512]{1,0:T(8,128)(2,1)S(1)} %collective-permute-done.19), channel_id=1, source_target_pairs={{0,1},{1,2},{2,3},{3,4},{4,5},{5,6},{6,7},{7,0},{8,9},{9,10},{10,1... | collective-permute-start | bytes 1966088 | tf_op jit(solution)/shard_map/ppermute | solution.py:24
  98.4 16.8 %collective-permute-start.21 = (bf16[640,512]{1,0:T(8,128)(2,1)S(1)}, bf16[640,512]{1,0:T(8,128)(2,1)S(1)}, u32[]{:S(2)}, u32[]{:S(2)}) collective-permute-start(bf16[640,512]{1,0:T(8,128)(2,1)S(1)} %collective-permute-done.17), channel_id=1, source_target_pairs={{0,7},{1,0},{2,1},{3,2},{4,3},{5,4},{6,5},{7,6},{8,15},{9,8},{10,9... | collective-permute-start | bytes 1966088 | tf_op jit(solution)/shard_map/ppermute | solution.py:24
  117.7 21.5 %collective-permute-start.22 = (bf16[256,1536]{1,0:T(8,128)(2,1)}, bf16[256,1536]{1,0:T(8,128)(2,1)}, u32[]{:S(2)}, u32[]{:S(2)}) collective-permute-start(bf16[256,1536]{1,0:T(8,128)(2,1)} %dynamic-slice_convert_fusion), channel_id=1, source_target_pairs={{0,8},{8,0},{1,9},{9,1},{2,10},{10,2},{3,11},{11,3},{4,12},{12,4},... | collective-permute-start | bytes 2359304 | tf_op jit(solution)/shard_map/ppermute | solution.py:24
  129.7 19.1 %all-to-all-start = ((bf16[16,16,1024]{2,1,0:T(8,128)(2,1)}), bf16[16,16,1024]{2,1,0:T(8,128)(2,1)}, u32[]{:S(2)}, u32[]{:S(2)}) async-start(bf16[16,16,1024]{2,1,0:T(8,128)(2,1)} %bitcast.78), calls=%async_computation | async-start | bytes 1048576 | tf_op jit(solution)/shard_map/all_to_all | solution.py:174
  148.8 16.5 %all-to-all-start.1 = ((bf16[16,16,1536]{2,1,0:T(8,128)(2,1)}), bf16[16,16,1536]{2,1,0:T(8,128)(2,1)S(1)}, u32[]{:S(2)}, u32[]{:S(2)}) async-start(bf16[16,16,1536]{2,1,0:T(8,128)(2,1)} %bitcast.77), calls=%async_computation.1 | async-start | bytes 1572864 | tf_op jit(solution)/shard_map/all_to_all | solution.py:174
  167.2 22.1 %all-to-all-start.3 = ((bf16[16,16,2560]{2,1,0:T(8,128)(2,1)}), bf16[16,16,2560]{2,1,0:T(8,128)(2,1)S(1)}, u32[]{:S(2)}, u32[]{:S(2)}) async-start(bf16[16,16,2560]{2,1,0:T(8,128)(2,1)} %broadcast_in_dim.99), calls=%async_computation.3 | async-start | bytes 2621440 | tf_op jit(solution)/shard_map/all_to_all | solution.py:66
  172.1 104.6 %all-gather.6.cloned.1.call-start = ((), (), s32[]{:S(2)}) async-start(), calls=%async_computation.5 | async-start | bytes 1052672 | tf_op jit(solution)/shard_map/all_gather | solution.py:192
  189.3 90.8 %collective-permute-start.23 = (bf16[256,2560]{1,0:T(8,128)(2,1)S(1)}, bf16[256,2560]{1,0:T(8,128)(2,1)S(1)}, u32[]{:S(2)}, u32[]{:S(2)}) collective-permute-start(bf16[256,2560]{1,0:T(8,128)(2,1)S(1)} %bitcast.75), channel_id=1, source_target_pairs={{0,8},{8,0},{1,9},{9,1},{2,10},{10,2},{3,11},{11,3},{4,12},{12,4},... | collective-permute-start | bytes 3932168 | tf_op jit(solution)/shard_map/ppermute | solution.py:24
  287.1 10.6 %collective-permute-start.25 = (bf16[512,128]{1,0:T(8,128)(2,1)S(1)}, bf16[512,128]{1,0:T(8,128)(2,1)S(1)}, u32[]{:S(2)}, u32[]{:S(2)}) collective-permute-start(bf16[512,128]{1,0:T(8,128)(2,1)S(1)} %convolution_convert_fusion), channel_id=1, source_target_pairs={{0,2},{1,3},{2,4},{3,5},{4,6},{5,7},{6,0},{7,1},{8,10},{9,11},{10,... | collective-permute-start | bytes 393224 | tf_op jit(solution)/shard_map/ppermute | solution.py:24
  291.4 9.7 %collective-permute-start.24 = (bf16[512,128]{1,0:T(8,128)(2,1)S(1)}, bf16[512,128]{1,0:T(8,128)(2,1)S(1)}, u32[]{:S(2)}, u32[]{:S(2)}) collective-permute-start(bf16[512,128]{1,0:T(8,128)(2,1)S(1)} %convolution_convert_fusion.1), channel_id=1, source_target_pairs={{0,6},{1,7},{2,0},{3,1},{4,2},{5,3},{6,4},{7,5},{8,14},{9,15},{10,... | collective-permute-start | bytes 393224 | tf_op jit(solution)/shard_map/ppermute | solution.py:24
  (20 other events, 154.8 us)
Sparse Core Ops, SparseCore 0:
  9.8 57.6 all-gather.3
  177.3 99.4 all-gather.5

commit v3 on v1

--- a/solution.py
+++ b/solution.py
@@ -72,10 +72,14 @@
     )
 
 
+def after(values, *others):
+    return lax.optimization_barrier((values, *others))[0]
+
+
 def split(value):
     high = lax.reduce_precision(value, 8, 7)
     middle = lax.reduce_precision(value - high, 8, 7)
-    return [t.astype(bf16) for t in (high, middle, value - high - middle)]
+    return high, middle, value - high - middle
 
 
 def whitened_kernel(core_ref, scale_ref, both_ref, q_ref, q_other_ref, inv_ref, inv_other_ref, out_ref, sums):
@@ -183,62 +187,53 @@
     early = over_plane(early_part)
     white_f, conj_f = white.astype(f32), conj.astype(f32)
     left_part = jnp.sum(white_f * white_f - conj_f * conj_f, axis=1)
-    strip = q_low.shape[1]
-    lines = height // strip
-    terms = jnp.stack(split(left_part)).reshape(3 * lines, strip)
-    terms = jnp.pad(terms, ((0, 16 - 3 * lines), (0, 0)))
-    q_all = lax.all_gather(jnp.concatenate([q_low, terms], axis=0), COLS, axis=0, tiled=True)
-    q_all = q_all.reshape(n_cols, width + 16, -1)
-    terms = q_all[:, width : width + 3 * lines].astype(f32).reshape(n_cols, 3, height)
-    left_grad = jnp.sum((terms[:, 0] + terms[:, 1]) + terms[:, 2], axis=0)
+    left_parts = from_everyone(left_part.reshape(-1, 128), COLS)
+    left_grad = jnp.sum(left_parts, axis=0).reshape(height)
     top_l = jnp.max(jnp.abs(left_grad))
     before_2, behind_2, _ = lax.optimization_barrier((before_2, behind_2, early_part))
     late_part = over_cores([(before, behind), (before, behind_2), (before_2, behind_2)])
     late = over_plane(late_part)
 
 
+    q_all = lax.all_gather(after(q_low, late_part), COLS, axis=0)
+
     top_r = jnp.maximum(jnp.max(jnp.abs(early)), jnp.max(jnp.abs(late)))
-    terms = jnp.stack(split(jnp.stack([top_r, top_l]))).reshape(1, 6)
-    note = jnp.broadcast_to(jnp.pad(terms, ((0, 0), (0, 122))), (piece, 128))
-    pieces = jnp.concatenate([early.astype(bf16), late.astype(bf16), note], axis=1)
-    mine = from_everyone(pieces, PLANE).reshape(half, -1)
+    lane = lax.broadcasted_iota(jnp.int32, (piece, 128), 1)
+    terms = split(jnp.where(lane < 3, top_r, top_l))
+    note = jnp.where(lane % 3 == 0, terms[0], jnp.where(lane % 3 == 1, terms[1], terms[2]))
+    pieces = jnp.concatenate([early.astype(bf16), late.astype(bf16), note.astype(bf16)], axis=1)
+    mine = from_everyone(pieces, PLANE)
+    notes = mine[:, :1, 5 * width :].astype(f32)
+    lane = lax.broadcasted_iota(jnp.int32, notes.shape, 2)
+    tops = [
+        jnp.max(jnp.sum(jnp.where((lane >= i) & (lane < i + 3), notes, 0.0), axis=2, keepdims=True), axis=0)
+        for i in (0, 3)
+    ]
+    lane = lax.broadcasted_iota(jnp.int32, (8, 128), 1)
+    tops = from_everyone(jnp.where(lane == 0, *tops), (CORE, COLS))
+    mine = mine[:, :, : 5 * width].reshape(half, -1)
     gram = in_core_order(mine, shift(mine, CORE, 1), 0)
-
-    def joined(terms):
-        terms = terms.astype(f32)
-        return (terms[:, 0] + terms[:, 1]) + terms[:, 2]
-
-    top_r, top_l = jnp.max(joined(gram[:, 5 * width : 5 * width + 6].reshape(width, 3, 2)), axis=0)
-    top_r = jnp.full((8, 128), top_r)
-    top_r = jnp.maximum(top_r, shift(top_r, COLS, n_cols // 2))[0, 0]
 
     def block(i, size=1):
         return gram[:, i * width : (i + size) * width]
 
-    def q_at(by, size=1):
-        rows = [
-            lax.dynamic_index_in_dim(q_all, (me + by + i + n_cols) % n_cols, 0, keepdims=False)[:width]
-            for i in range(size)
-        ]
-        return jnp.concatenate(rows, axis=0)
-
-    note = jnp.pad(jnp.stack(split(top_r))[:, None], ((0, 13), (0, strip - 1)))
+    def times(i, by):
+        rows = [lax.dynamic_index_in_dim(q_all, (me + j + n_cols) % n_cols, 0, keepdims=False) for j in by]
+        return dot(block(i, len(by)), jnp.concatenate(rows, axis=0), 1, 0)
+
+    def turned_times(i, by):
+        rows = lax.dynamic_index_in_dim(q_all, (me + by + n_cols) % n_cols, 0, keepdims=False)
+        return dot(block(i), rows, 0, 0)
 
     def sent(value, by):
-        return shift(jnp.concatenate([value.astype(bf16), note], axis=0), COLS, by)
-
-    got = [
-        sent(dot(block(4), q_at(2), 1, 0), -2),
-        sent(dot(block(3), q_at(-1), 0, 0), 2),
-        sent(dot(block(2, 2), q_at(1, 2), 1, 0), -1),
-        sent(dot(block(1), q_at(0), 0, 0) + dot(block(2), q_at(-1), 0, 0), 1),
-    ]
-    product = dot(block(0, 2), q_at(0, 2), 1, 0)
-    for value in got:
-        product = product + value[:width].astype(f32)
-        top_r = jnp.maximum(top_r, joined(value[width : width + 3, :1].T)[0])
-    scale_r = learn_rate / (top_r + epsilon)
-    scale_l = learn_rate / (top_l + epsilon)
+        return shift(value.astype(bf16), COLS, by).astype(f32)
+
+    values = [turned_times(3, -1), times(4, (2,)), times(2, (1, 2)), turned_times(1, 0) + turned_times(2, -1)]
+    got = [sent(value, by) for value, by in zip(values, (2, -2, -1, 1), strict=True)]
+    product = times(0, (0, 1))
+    tops = jnp.max(after(tops, values[3], product), axis=(0, 1))
+    scale_r, scale_l = (learn_rate / (tops[i] + epsilon) for i in range(2))
+    product = product + ((got[0] + got[1]) + (got[2] + got[3]))
     left_new = left_factor - scale_l * left_grad * left_factor
     q_new = q_right - scale_r * product
     return (left_new, q_new)

time: 234 us -> 241 us (1.030)
  waiting for transfers between devices: 62.6 us -> 97.9 us
  between operations: 29.3 us -> 17.4 us
  blocking collectives: 23.3 us -> 13 us
  matrix products: 13.9 us -> 7.42 us
  starting transfers between devices: 51.1 us -> 54.8 us
  local copies, waits for them, and re-layouts: 23.4 us -> 20.6 us
    all_gather x1, waiting for transfers between devices: 0.01 us -> 19.3 us  [body(): q_all = lax.all_gather(after(q_low, late_part), COLS, axis=0)]
    all_to_all x0 -> x2, waiting for transfers between devices: none -> 17.2 us  [from_everyone(): return lax.all_to_all(copies, axes, 0, 0, tiled=True)]
    all_to_all x1, blocking collectives: 23.3 us -> 13 us  [from_everyone(): return lax.all_to_all(copies, axes, 0, 0, tiled=True)]
    all_to_all x0 -> x2, starting transfers between devices: none -> 9.21 us  [from_everyone(): return lax.all_to_all(copies, axes, 0, 0, tiled=True)]
    dot_general x11, matrix products: 13.9 us -> 7.42 us  [dot(): lax.dot_general(left, right, (((left_dim,), (right_dim,)), ((), ())), pre...]
    ppermute x29 -> x28, starting transfers between devices: 38.1 us -> 33.4 us  [shift(): lax.ppermute(value, axis, [(i, (i + by) % size) for i in range(size)])]
    slice x6 -> x2, local copies, waits for them, and re-layouts: 4.15 us -> 0.71 us  [the longest x1 0.59 us: body(): scale_r, scale_l = (learn_rate / (tops[i] + epsilon) for i in range(2))]
    ppermute x29 -> x28, waiting for transfers between devices: 38.3 us -> 38.7 us  [shift(): lax.ppermute(value, axis, [(i, (i + by) % size) for i in range(size)])]
  transfers between devices with their start and end apart: 33 -> 34, of which waited for: 13 -> 16; matrix products, arithmetic and copies ran while one was open for 18% -> 16% of each run, Pallas kernels for 0% -> 0%
where the time goes in v3:
time: 241 us; the launch traced here: 240 us
  waiting for transfers between devices  97.9 us (41%)
  starting transfers between devices  54.8 us (23%)
  local copies, waits for them, and re-layouts  20.6 us (9%)
  other arithmetic  19.2 us (8%)
  between operations  17.4 us (7%)
  blocking collectives  13 us (5%)
  Pallas kernels  9.33 us (4%)
  matrix products  7.42 us (3%)
    ppermute x28, waiting for transfers between devices, shift(): lax.ppermute(value, axis, [(i, (i + by) % size) for i in range(size)])  38.7 us
    ppermute x28, starting transfers between devices, shift(): lax.ppermute(value, axis, [(i, (i + by) % size) for i in range(size)])  33.4 us
    all_gather x1, waiting for transfers between devices, body(): q_all = lax.all_gather(after(q_low, late_part), COLS, axis=0)  19.3 us
    all_to_all x2, waiting for transfers between devices, from_everyone(): return lax.all_to_all(copies, axes, 0, 0, tiled=True)  17.2 us
    all_to_all x2, waiting for transfers between devices, over_plane(): parts = lax.all_to_all(part, PLANE, 0, 0, tiled=True)  16.6 us
    all_to_all x1, blocking collectives, from_everyone(): return lax.all_to_all(copies, axes, 0, 0, tiled=True)  13 us
    all_to_all x2, starting transfers between devices, over_plane(): parts = lax.all_to_all(part, PLANE, 0, 0, tiled=True)  12.1 us
    pallas_call x1, Pallas kernels, whitened(): pl.pallas_call(whitened_kernel, grid=(depth // deep,), out_shape=jax.Shap...  9.33 us
  transfers between devices with their start and end apart: 34, of which 16 were waited for; matrix products, arithmetic and copies ran while one was open for 16% of the time, Pallas kernels for 0%

profile of v3, /device:TPU:2, one launch (start us, length us, event | category | flops | bytes accessed | tf_op | source)
XLA Modules:
  0.0 239.6 jit_solution(13408708935305447011)
XLA Ops:
  19.7 2.2 collective-permute-start.3
  27.8 2.7 %collective-permute-start.5 = (bf16[4,256,256]{2,1,0:T(8,128)(2,1)S(1)}, bf16[4,256,256]{2,1,0:T(8,128)(2,1)}, u32[]{:S(2)}, u32[]{:S(2)}) collective-permute-start(bf16[4,256,256]{2,1,0:T(8,128)(2,1)S(1)} %constant_dynamic-update-slice_fusion.4), channel_id=1, source_target_pairs={{0,192},{64,0},{128,64},{192,128},{1,193},{65,1},{129,65},{193,129... | collective-permute-start | bytes 1572872 | tf_op jit(solution)/shard_map/ppermute | solution.py:24
  33.2 4.3 %collective-permute-done.12 = bf16[4,256,256]{2,1,0:T(8,128)(2,1)} collective-permute-done((bf16[4,256,256]{2,1,0:T(8,128)(2,1)S(1)}, bf16[4,256,256]{2,1,0:T(8,128)(2,1)}, u32[]{:S(2)}, u32[]{:S(2)}) %collective-permute-start.12) | collective-permute-done | bytes 524320 | tf_op jit(solution)/shard_map/ppermute | solution.py:24
  44.5 2.7 %collective-permute-start.7 = (bf16[2,256,256]{2,1,0:T(8,128)(2,1)S(1)}, bf16[2,256,256]{2,1,0:T(8,128)(2,1)S(1)}, u32[]{:S(2)}, u32[]{:S(2)}) collective-permute-start(bf16[2,256,256]{2,1,0:T(8,128)(2,1)S(1)} %slice.96), channel_id=1, source_target_pairs={{0,192},{64,0},{128,64},{192,128},{1,193},{65,1},{129,65},{193,129... | collective-permute-start | bytes 786440 | tf_op jit(solution)/shard_map/ppermute | solution.py:24
  56.2 2.9 %collective-permute-done.16.inv_other_ref = bf16[4096,256]{1,0:T(8,128)(2,1)} collective-permute-done((bf16[4096,256]{1,0:T(8,128)(2,1)}, bf16[4096,256]{1,0:T(8,128)(2,1)}, u32[]{:S(2)}, u32[]{:S(2)}) %collective-permute-start.16) | collective-permute-done | bytes 2097184 | tf_op jit(solution)/shard_map/ppermute | solution.py:24
  59.1 3.0 %collective-permute-done.8.q_other_ref = bf16[4096,256]{1,0:T(8,128)(2,1)} collective-permute-done((bf16[4096,256]{1,0:T(8,128)(2,1)S(1)}, bf16[4096,256]{1,0:T(8,128)(2,1)}, u32[]{:S(2)}, u32[]{:S(2)}) %collective-permute-start.8) | collective-permute-done | bytes 2097184 | tf_op jit(solution)/shard_map/ppermute | solution.py:24
  62.1 5.4 %all-gather.4.cloned.1.call-done.both_ref = bf16[512,4096]{1,0:T(8,128)(2,1)} async-done(((bf16[512,512]{1,0:T(8,128)(2,1)}), bf16[512,4096]{1,0:T(8,128)(2,1)}) %all-gather.4.cloned.1.call-update) | async-done | bytes 4194320 | tf_op jit(solution)/shard_map/all_gather | solution.py:140
  67.5 9.3 %whitened.1 = bf16[512,512]{1,0:T(8,128)(2,1)} custom-call(s32[1]{0:T(128)} %bitcast.core_ref, f32[512,1]{1,0:T(8,128)} %copy.72.scale_ref, bf16[512,4096]{1,0:T(8,128)(2,1)} %all-gather.4.cloned.1.call-done.both_ref, bf16[4096,256]{1,0:T(8,128)(2,1)} %bitcast.86, bf16[4096,256]{1,0:T(8,128)(2,1)} %collective-permute-done.8.q_other_ref, ...), custom_call_target="tpu_custom_call" | custom-call | flops 2147483648 | bytes 12582912 | tf_op jit(solution)/shard_map/whitened/pallas_call | solution.py:111
  81.5 9.1 %collective-permute-done.17 = bf16[512,512]{1,0:T(8,128)(2,1)S(1)} collective-permute-done((bf16[512,512]{1,0:T(8,128)(2,1)}, bf16[512,512]{1,0:T(8,128)(2,1)S(1)}, u32[]{:S(2)}, u32[]{:S(2)}) %collective-permute-start.17) | collective-permute-done | bytes 524320 | tf_op jit(solution)/shard_map/ppermute | solution.py:24
  92.9 3.2 %collective-permute-start.21 = (bf16[512,512]{1,0:T(8,128)(2,1)S(1)}, bf16[512,512]{1,0:T(8,128)(2,1)S(1)}, u32[]{:S(2)}, u32[]{:S(2)}) collective-permute-start(bf16[512,512]{1,0:T(8,128)(2,1)S(1)} %collective-permute-done.17), channel_id=1, source_target_pairs={{0,7},{1,0},{2,1},{3,2},{4,3},{5,4},{6,5},{7,6},{8,15},{9,8},{10,9... | collective-permute-start | bytes 1572872 | tf_op jit(solution)/shard_map/ppermute | solution.py:24
  97.5 9.3 %collective-permute-done.20 = bf16[512,512]{1,0:T(8,128)(2,1)S(1)} collective-permute-done((bf16[512,512]{1,0:T(8,128)(2,1)S(1)}, bf16[512,512]{1,0:T(8,128)(2,1)S(1)}, u32[]{:S(2)}, u32[]{:S(2)}) %collective-permute-start.20) | collective-permute-done | bytes 524320 | tf_op jit(solution)/shard_map/ppermute | solution.py:24
  109.2 13.0 %all_to_all.25 = f32[8,2,128]{2,1,0:T(2,128)S(1)} all-to-all(f32[8,2,128]{2,1,0:T(2,128)S(1)} %broadcast_in_dim.126), channel_id=1, replica_groups=mesh['rows_0'=4,'rows_1'=4,'rows_2'=2,'cols'=8] {'cols'}, dimensions={0} | all-to-all | bytes 16384 | tf_op jit(solution)/shard_map/all_to_all | solution.py:66
  122.2 7.3 %all-to-all-start = ((bf16[16,16,1024]{2,1,0:T(8,128)(2,1)}), bf16[16,16,1024]{2,1,0:T(8,128)(2,1)}, u32[]{:S(2)}, u32[]{:S(2)}) async-start(bf16[16,16,1024]{2,1,0:T(8,128)(2,1)} %bitcast.90), calls=%async_computation | async-start | bytes 1048576 | tf_op jit(solution)/shard_map/all_to_all | solution.py:183
  129.5 2.2 add_convert_fusion
  131.7 7.3 %all-to-all-done = bf16[16,16,1024]{2,1,0:T(8,128)(2,1)} async-done(((bf16[16,16,1024]{2,1,0:T(8,128)(2,1)}), bf16[16,16,1024]{2,1,0:T(8,128)(2,1)}, u32[]{:S(2)}, u32[]{:S(2)}) %all-to-all-start) | async-done | bytes 524320 | tf_op jit(solution)/shard_map/all_to_all | solution.py:183
  139.0 4.8 %all-to-all-start.1 = ((bf16[16,16,1536]{2,1,0:T(8,128)(2,1)}), bf16[16,16,1536]{2,1,0:T(8,128)(2,1)S(1)}, u32[]{:S(2)}, u32[]{:S(2)}) async-start(bf16[16,16,1536]{2,1,0:T(8,128)(2,1)} %bitcast.89), calls=%async_computation.1 | async-start | bytes 1572864 | tf_op jit(solution)/shard_map/all_to_all | solution.py:183
  146.2 9.3 %all-to-all-done.1 = bf16[16,16,1536]{2,1,0:T(8,128)(2,1)S(1)} async-done(((bf16[16,16,1536]{2,1,0:T(8,128)(2,1)}), bf16[16,16,1536]{2,1,0:T(8,128)(2,1)S(1)}, u32[]{:S(2)}, u32[]{:S(2)}) %all-to-all-start.1) | async-done | bytes 786464 | tf_op jit(solution)/shard_map/all_to_all | solution.py:183
  160.7 5.0 %all-to-all-start.3 = ((bf16[16,16,2688]{2,1,0:T(8,128)(2,1)}), bf16[16,16,2688]{2,1,0:T(8,128)(2,1)S(1)}, u32[]{:S(2)}, u32[]{:S(2)}) async-start(bf16[16,16,2688]{2,1,0:T(8,128)(2,1)} %broadcast_in_dim.128), calls=%async_computation.3 | async-start | bytes 2752512 | tf_op jit(solution)/shard_map/all_to_all | solution.py:66
  166.4 17.2 %all-to-all-done.3 = bf16[16,16,2688]{2,1,0:T(8,128)(2,1)S(1)} async-done(((bf16[16,16,2688]{2,1,0:T(8,128)(2,1)}), bf16[16,16,2688]{2,1,0:T(8,128)(2,1)S(1)}, u32[]{:S(2)}, u32[]{:S(2)}) %all-to-all-start.3) | async-done | bytes 1376288 | tf_op jit(solution)/shard_map/all_to_all | solution.py:66
  184.0 19.3 %all-gather.6.cloned.1.call-done = bf16[4096,128]{1,0:T(8,128)(2,1)} async-done(((bf16[512,128]{1,0:T(8,128)(2,1)}), bf16[4096,128]{1,0:T(8,128)(2,1)}) %all-gather.6.cloned.1.call-update) | async-done | bytes 1048592 | tf_op jit(solution)/shard_map/all_gather | solution.py:198
  207.7 4.3 %all-to-all-start.4 = ((f32[16,8,128]{2,1,0:T(8,128)}), f32[16,8,128]{2,1,0:T(8,128)S(1)}, u32[]{:S(2)}, u32[]{:S(2)}) async-start(f32[16,8,128]{2,1,0:T(8,128)} %broadcast_in_dim.132), calls=%async_computation.4 | async-start | bytes 131072 | tf_op jit(solution)/shard_map/all_to_all | solution.py:66
  216.6 2.9 %collective-permute-start.24 = (bf16[512,128]{1,0:T(8,128)(2,1)S(1)}, bf16[512,128]{1,0:T(8,128)(2,1)S(1)}, u32[]{:S(2)}, u32[]{:S(2)}) collective-permute-start(bf16[512,128]{1,0:T(8,128)(2,1)S(1)} %convolution_convert_fusion.1), channel_id=1, source_target_pairs={{0,2},{1,3},{2,4},{3,5},{4,6},{5,7},{6,0},{7,1},{8,10},{9,11},{10,... | collective-permute-start | bytes 393224 | tf_op jit(solution)/shard_map/ppermute | solution.py:24
  227.2 2.6 %collective-permute-done.25 = bf16[512,128]{1,0:T(8,128)(2,1)S(1)} collective-permute-done((bf16[512,128]{1,0:T(8,128)(2,1)S(1)}, bf16[512,128]{1,0:T(8,128)(2,1)S(1)}, u32[]{:S(2)}, u32[]{:S(2)}) %collective-permute-start.25) | collective-permute-done | bytes 131104 | tf_op jit(solution)/shard_map/ppermute | solution.py:24
  229.8 2.1 collective-permute-done.26
  (157 shorter events, 70.6 us)
Async XLA Ops:
  7.2 60.3 %all-gather.4.cloned.1.call-start = ((), (), s32[]{:S(2)}) async-start(), calls=%async_computation.5 | async-start | bytes 4718592 | tf_op jit(solution)/shard_map/all_gather | solution.py:140
  13.5 8.6 %collective-permute-start.10 = (bf16[256,256]{0,1:T(8,128)(2,1)S(1)}, bf16[256,256]{0,1:T(8,128)(2,1)S(1)}, u32[]{:S(2)}, u32[]{:S(2)}) collective-permute-start(bf16[256,256]{0,1:T(8,128)(2,1)S(1)} %maximum_select_fusion.4), channel_id=1, source_target_pairs={{0,192},{64,0},{128,64},{192,128},{1,193},{65,1},{129,65},{193,129... | collective-permute-start | bytes 393224 | tf_op jit(solution)/shard_map/ppermute | solution.py:24
  22.8 14.7 %collective-permute-start.12 = (bf16[4,256,256]{2,1,0:T(8,128)(2,1)S(1)}, bf16[4,256,256]{2,1,0:T(8,128)(2,1)}, u32[]{:S(2)}, u32[]{:S(2)}) collective-permute-start(bf16[4,256,256]{2,1,0:T(8,128)(2,1)S(1)} %constant_dynamic-update-slice_fusion), channel_id=1, source_target_pairs={{0,16},{16,32},{32,48},{48,0},{1,17},{17,33},{33,49},{49,1},{2,18}... | collective-permute-start | bytes 1572872 | tf_op jit(solution)/shard_map/ppermute | solution.py:24
  24.4 15.7 %collective-permute-start.13 = (bf16[4,256,256]{2,1,0:T(8,128)(2,1)S(1)}, bf16[4,256,256]{2,1,0:T(8,128)(2,1)}, u32[]{:S(2)}, u32[]{:S(2)}) collective-permute-start(bf16[4,256,256]{2,1,0:T(8,128)(2,1)S(1)} %constant_dynamic-update-slice_fusion), channel_id=1, source_target_pairs={{0,48},{16,0},{32,16},{48,32},{1,49},{17,1},{33,17},{49,33},{2,50}... | collective-permute-start | bytes 1572872 | tf_op jit(solution)/shard_map/ppermute | solution.py:24
  27.2 14.4 %collective-permute-start.4 = (bf16[4,256,256]{2,1,0:T(8,128)(2,1)S(1)}, bf16[4,256,256]{2,1,0:T(8,128)(2,1)}, u32[]{:S(2)}, u32[]{:S(2)}) collective-permute-start(bf16[4,256,256]{2,1,0:T(8,128)(2,1)S(1)} %constant_dynamic-update-slice_fusion.4), channel_id=1, source_target_pairs={{0,64},{64,128},{128,192},{192,0},{1,65},{65,129},{129,193},{193,1... | collective-permute-start | bytes 1572872 | tf_op jit(solution)/shard_map/ppermute | solution.py:24
  27.8 15.7 %collective-permute-start.5 = (bf16[4,256,256]{2,1,0:T(8,128)(2,1)S(1)}, bf16[4,256,256]{2,1,0:T(8,128)(2,1)}, u32[]{:S(2)}, u32[]{:S(2)}) collective-permute-start(bf16[4,256,256]{2,1,0:T(8,128)(2,1)S(1)} %constant_dynamic-update-slice_fusion.4), channel_id=1, source_target_pairs={{0,192},{64,0},{128,64},{192,128},{1,193},{65,1},{129,65},{193,129... | collective-permute-start | bytes 1572872 | tf_op jit(solution)/shard_map/ppermute | solution.py:24
  38.5 14.7 %collective-permute-start.14 = (bf16[2,256,256]{2,1,0:T(8,128)(2,1)S(1)}, bf16[2,256,256]{2,1,0:T(8,128)(2,1)S(1)}, u32[]{:S(2)}, u32[]{:S(2)}) collective-permute-start(bf16[2,256,256]{2,1,0:T(8,128)(2,1)S(1)} %slice.98), channel_id=1, source_target_pairs={{0,16},{16,32},{32,48},{48,0},{1,17},{17,33},{33,49},{49,1},{2,18}... | collective-permute-start | bytes 786440 | tf_op jit(solution)/shard_map/ppermute | solution.py:24
  41.0 12.9 %collective-permute-start.15 = (bf16[2,256,256]{2,1,0:T(8,128)(2,1)S(1)}, bf16[2,256,256]{2,1,0:T(8,128)(2,1)S(1)}, u32[]{:S(2)}, u32[]{:S(2)}) collective-permute-start(bf16[2,256,256]{2,1,0:T(8,128)(2,1)S(1)} %slice.99), channel_id=1, source_target_pairs={{0,48},{16,0},{32,16},{48,32},{1,49},{17,1},{33,17},{49,33},{2,50}... | collective-permute-start | bytes 786440 | tf_op jit(solution)/shard_map/ppermute | solution.py:24
  42.6 12.0 %collective-permute-start.6 = (bf16[2,256,256]{2,1,0:T(8,128)(2,1)S(1)}, bf16[2,256,256]{2,1,0:T(8,128)(2,1)S(1)}, u32[]{:S(2)}, u32[]{:S(2)}) collective-permute-start(bf16[2,256,256]{2,1,0:T(8,128)(2,1)S(1)} %slice.95), channel_id=1, source_target_pairs={{0,64},{64,128},{128,192},{192,0},{1,65},{65,129},{129,193},{193,1... | collective-permute-start | bytes 786440 | tf_op jit(solution)/shard_map/ppermute | solution.py:24
  44.5 10.2 %collective-permute-start.7 = (bf16[2,256,256]{2,1,0:T(8,128)(2,1)S(1)}, bf16[2,256,256]{2,1,0:T(8,128)(2,1)S(1)}, u32[]{:S(2)}, u32[]{:S(2)}) collective-permute-start(bf16[2,256,256]{2,1,0:T(8,128)(2,1)S(1)} %slice.96), channel_id=1, source_target_pairs={{0,192},{64,0},{128,64},{192,128},{1,193},{65,1},{129,65},{193,129... | collective-permute-start | bytes 786440 | tf_op jit(solution)/shard_map/ppermute | solution.py:24
  76.8 13.7 %collective-permute-start.17 = (bf16[512,512]{1,0:T(8,128)(2,1)}, bf16[512,512]{1,0:T(8,128)(2,1)S(1)}, u32[]{:S(2)}, u32[]{:S(2)}) collective-permute-start(bf16[512,512]{1,0:T(8,128)(2,1)} %whitened.1), channel_id=1, source_target_pairs={{0,7},{1,0},{2,1},{3,2},{4,3},{5,4},{6,5},{7,6},{8,15},{9,8},{10,9... | collective-permute-start | bytes 1572872 | tf_op jit(solution)/shard_map/ppermute | solution.py:24
  78.2 14.6 %collective-permute-start.19 = (bf16[512,512]{1,0:T(8,128)(2,1)}, bf16[512,512]{1,0:T(8,128)(2,1)S(1)}, u32[]{:S(2)}, u32[]{:S(2)}) collective-permute-start(bf16[512,512]{1,0:T(8,128)(2,1)} %whitened.1), channel_id=1, source_target_pairs={{0,1},{1,2},{2,3},{3,4},{4,5},{5,6},{6,7},{7,0},{8,9},{9,10},{10,1... | collective-permute-start | bytes 1572872 | tf_op jit(solution)/shard_map/ppermute | solution.py:24
  92.9 13.9 %collective-permute-start.20 = (bf16[512,512]{1,0:T(8,128)(2,1)S(1)}, bf16[512,512]{1,0:T(8,128)(2,1)S(1)}, u32[]{:S(2)}, u32[]{:S(2)}) collective-permute-start(bf16[512,512]{1,0:T(8,128)(2,1)S(1)} %collective-permute-done.19), channel_id=1, source_target_pairs={{0,1},{1,2},{2,3},{3,4},{4,5},{5,6},{6,7},{7,0},{8,9},{9,10},{10,1... | collective-permute-start | bytes 1572872 | tf_op jit(solution)/shard_map/ppermute | solution.py:24
  92.9 13.9 %collective-permute-start.21 = (bf16[512,512]{1,0:T(8,128)(2,1)S(1)}, bf16[512,512]{1,0:T(8,128)(2,1)S(1)}, u32[]{:S(2)}, u32[]{:S(2)}) collective-permute-start(bf16[512,512]{1,0:T(8,128)(2,1)S(1)} %collective-permute-done.17), channel_id=1, source_target_pairs={{0,7},{1,0},{2,1},{3,2},{4,3},{5,4},{6,5},{7,6},{8,15},{9,8},{10,9... | collective-permute-start | bytes 1572872 | tf_op jit(solution)/shard_map/ppermute | solution.py:24
  109.0 20.5 %collective-permute-start.22 = (bf16[256,1536]{1,0:T(8,128)(2,1)}, bf16[256,1536]{1,0:T(8,128)(2,1)}, u32[]{:S(2)}, u32[]{:S(2)}) collective-permute-start(bf16[256,1536]{1,0:T(8,128)(2,1)} %dynamic-slice_convert_fusion), channel_id=1, source_target_pairs={{0,8},{8,0},{1,9},{9,1},{2,10},{10,2},{3,11},{11,3},{4,12},{12,4},... | collective-permute-start | bytes 2359304 | tf_op jit(solution)/shard_map/ppermute | solution.py:24
  122.2 16.8 %all-to-all-start = ((bf16[16,16,1024]{2,1,0:T(8,128)(2,1)}), bf16[16,16,1024]{2,1,0:T(8,128)(2,1)}, u32[]{:S(2)}, u32[]{:S(2)}) async-start(bf16[16,16,1024]{2,1,0:T(8,128)(2,1)} %bitcast.90), calls=%async_computation | async-start | bytes 1048576 | tf_op jit(solution)/shard_map/all_to_all | solution.py:183
  139.0 16.5 %all-to-all-start.1 = ((bf16[16,16,1536]{2,1,0:T(8,128)(2,1)}), bf16[16,16,1536]{2,1,0:T(8,128)(2,1)S(1)}, u32[]{:S(2)}, u32[]{:S(2)}) async-start(bf16[16,16,1536]{2,1,0:T(8,128)(2,1)} %bitcast.89), calls=%async_computation.1 | async-start | bytes 1572864 | tf_op jit(solution)/shard_map/all_to_all | solution.py:183
  160.7 22.9 %all-to-all-start.3 = ((bf16[16,16,2688]{2,1,0:T(8,128)(2,1)}), bf16[16,16,2688]{2,1,0:T(8,128)(2,1)S(1)}, u32[]{:S(2)}, u32[]{:S(2)}) async-start(bf16[16,16,2688]{2,1,0:T(8,128)(2,1)} %broadcast_in_dim.128), calls=%async_computation.3 | async-start | bytes 2752512 | tf_op jit(solution)/shard_map/all_to_all | solution.py:66
  165.7 37.6 %all-gather.6.cloned.1.call-start = ((), (), s32[]{:S(2)}) async-start(), calls=%async_computation.6 | async-start | bytes 1179648 | tf_op jit(solution)/shard_map/all_gather | solution.py:198
  183.8 28.2 %collective-permute-start.23 = (bf16[256,2560]{1,0:T(8,128)(2,1)S(1)}, bf16[256,2560]{1,0:T(8,128)(2,1)}, u32[]{:S(2)}, u32[]{:S(2)}) collective-permute-start(bf16[256,2560]{1,0:T(8,128)(2,1)S(1)} %bitcast.87), channel_id=1, source_target_pairs={{0,8},{8,0},{1,9},{9,1},{2,10},{10,2},{3,11},{11,3},{4,12},{12,4},... | collective-permute-start | bytes 3932168 | tf_op jit(solution)/shard_map/ppermute | solution.py:24
  207.7 16.9 %all-to-all-start.4 = ((f32[16,8,128]{2,1,0:T(8,128)}), f32[16,8,128]{2,1,0:T(8,128)S(1)}, u32[]{:S(2)}, u32[]{:S(2)}) async-start(f32[16,8,128]{2,1,0:T(8,128)} %broadcast_in_dim.132), calls=%async_computation.4 | async-start | bytes 131072 | tf_op jit(solution)/shard_map/all_to_all | solution.py:66
  216.6 10.6 %collective-permute-start.24 = (bf16[512,128]{1,0:T(8,128)(2,1)S(1)}, bf16[512,128]{1,0:T(8,128)(2,1)S(1)}, u32[]{:S(2)}, u32[]{:S(2)}) collective-permute-start(bf16[512,128]{1,0:T(8,128)(2,1)S(1)} %convolution_convert_fusion.1), channel_id=1, source_target_pairs={{0,2},{1,3},{2,4},{3,5},{4,6},{5,7},{6,0},{7,1},{8,10},{9,11},{10,... | collective-permute-start | bytes 393224 | tf_op jit(solution)/shard_map/ppermute | solution.py:24
  219.8 10.0 %collective-permute-start.25 = (bf16[512,128]{1,0:T(8,128)(2,1)S(1)}, bf16[512,128]{1,0:T(8,128)(2,1)S(1)}, u32[]{:S(2)}, u32[]{:S(2)}) collective-permute-start(bf16[512,128]{1,0:T(8,128)(2,1)S(1)} %convolution_convert_fusion), channel_id=1, source_target_pairs={{0,6},{1,7},{2,0},{3,1},{4,2},{5,3},{6,4},{7,5},{8,14},{9,15},{10,... | collective-permute-start | bytes 393224 | tf_op jit(solution)/shard_map/ppermute | solution.py:24
  221.7 10.3 %collective-permute-start.26 = (bf16[512,128]{1,0:T(8,128)(2,1)S(1)}, bf16[512,128]{1,0:T(8,128)(2,1)S(1)}, u32[]{:S(2)}, u32[]{:S(2)}) collective-permute-start(bf16[512,128]{1,0:T(8,128)(2,1)S(1)} %convolution_convert_fusion.2), channel_id=1, source_target_pairs={{0,7},{1,0},{2,1},{3,2},{4,3},{5,4},{6,5},{7,6},{8,15},{9,8},{10,9... | collective-permute-start | bytes 393224 | tf_op jit(solution)/shard_map/ppermute | solution.py:24
  (16 other events, 117.7 us)
Sparse Core Ops, SparseCore 0:
  9.8 57.6 all-gather.3
  168.3 34.9 all-gather.5

commit v4 on v3

--- a/solution.py
+++ b/solution.py
@@ -107,7 +107,7 @@
 
 def whitened(core, scale, both, *factors):
     (rows, depth), half = both.shape, factors[0].shape[1]
-    deep = min(512, depth)
+    deep = min(1024, depth)
     return pl.pallas_call(
         whitened_kernel,
         grid=(depth // deep,),
@@ -120,6 +120,7 @@
         ],
         out_specs=pl.BlockSpec((rows, 2 * half), lambda k: (0, 0)),
         scratch_shapes=[pltpu.VMEM((2, rows, half), f32)],
+        compiler_params=pltpu.CompilerParams(vmem_limit_bytes=16 * 2**20),
         cost_estimate=pl.CostEstimate(
             flops=4 * rows * depth * half, bytes_accessed=2 * depth * (rows + 4 * half), transcendentals=0
         ),
@@ -198,19 +199,14 @@
     q_all = lax.all_gather(after(q_low, late_part), COLS, axis=0)
 
     top_r = jnp.maximum(jnp.max(jnp.abs(early)), jnp.max(jnp.abs(late)))
-    lane = lax.broadcasted_iota(jnp.int32, (piece, 128), 1)
-    terms = split(jnp.where(lane < 3, top_r, top_l))
-    note = jnp.where(lane % 3 == 0, terms[0], jnp.where(lane % 3 == 1, terms[1], terms[2]))
+    row, lane = (lax.broadcasted_iota(jnp.int32, (piece, 128), i) for i in range(2))
+    terms = split(lax.optimization_barrier(jnp.where(lane < 64, top_r, top_l)))
+    note = jnp.where(row == 0, terms[0], jnp.where(row == 1, terms[1], terms[2]))
     pieces = jnp.concatenate([early.astype(bf16), late.astype(bf16), note.astype(bf16)], axis=1)
     mine = from_everyone(pieces, PLANE)
-    notes = mine[:, :1, 5 * width :].astype(f32)
-    lane = lax.broadcasted_iota(jnp.int32, notes.shape, 2)
-    tops = [
-        jnp.max(jnp.sum(jnp.where((lane >= i) & (lane < i + 3), notes, 0.0), axis=2, keepdims=True), axis=0)
-        for i in (0, 3)
-    ]
-    lane = lax.broadcasted_iota(jnp.int32, (8, 128), 1)
-    tops = from_everyone(jnp.where(lane == 0, *tops), (CORE, COLS))
+    notes = mine[:, :, 5 * width :].astype(f32)
+    tops = jnp.max((notes[:, 0:1] + notes[:, 1:2]) + notes[:, 2:3], axis=0)
+    tops = from_everyone(jnp.broadcast_to(tops, (8, 128)), (CORE, COLS))
     mine = mine[:, :, : 5 * width].reshape(half, -1)
     gram = in_core_order(mine, shift(mine, CORE, 1), 0)
 
@@ -232,7 +228,7 @@
     got = [sent(value, by) for value, by in zip(values, (2, -2, -1, 1), strict=True)]
     product = times(0, (0, 1))
     tops = jnp.max(after(tops, values[3], product), axis=(0, 1))
-    scale_r, scale_l = (learn_rate / (tops[i] + epsilon) for i in range(2))
+    scale_r, scale_l = (learn_rate / (tops[i] + epsilon) for i in (0, 64))
     product = product + ((got[0] + got[1]) + (got[2] + got[3]))
     left_new = left_factor - scale_l * left_grad * left_factor
     q_new = q_right - scale_r * product

time: 241 us -> 236 us (0.979)
  other arithmetic: 19.2 us -> 14.3 us
  Pallas kernels: 9.33 us -> 5.45 us
  waiting for transfers between devices: 97.9 us -> 101 us
    pallas_call x1, Pallas kernels: 9.33 us -> 5.45 us  [whitened(): pl.pallas_call(whitened_kernel, grid=(depth // deep,), out_shape=jax.Shap...]
    ppermute x28, waiting for transfers between devices: 38.7 us -> 41.2 us  [shift(): lax.ppermute(value, axis, [(i, (i + by) % size) for i in range(size)])]
  transfers between devices with their start and end apart: 34 -> 34, of which waited for: 16 -> 16; matrix products, arithmetic and copies ran while one was open for 16% -> 14% of each run, Pallas kernels for 0% -> 0%
where the time goes in v4:
time: 236 us; the launch traced here: 234 us
  waiting for transfers between devices  101 us (43%)
  starting transfers between devices  54.8 us (23%)
  local copies, waits for them, and re-layouts  22.1 us (9%)
  between operations  17.4 us (7%)
  other arithmetic  14.3 us (6%)
  blocking collectives  13 us (6%)
  matrix products  6.38 us (3%)
  Pallas kernels  5.45 us (2%)
    ppermute x28, waiting for transfers between devices, shift(): lax.ppermute(value, axis, [(i, (i + by) % size) for i in range(size)])  41.2 us
    ppermute x28, starting transfers between devices, shift(): lax.ppermute(value, axis, [(i, (i + by) % size) for i in range(size)])  33.5 us
    all_gather x1, waiting for transfers between devices, body(): q_all = lax.all_gather(after(q_low, late_part), COLS, axis=0)  19.9 us
    all_to_all x2, waiting for transfers between devices, from_everyone(): return lax.all_to_all(copies, axes, 0, 0, tiled=True)  17.2 us
    all_to_all x2, waiting for transfers between devices, over_plane(): parts = lax.all_to_all(part, PLANE, 0, 0, tiled=True)  16.6 us
    all_to_all x1, blocking collectives, from_everyone(): return lax.all_to_all(copies, axes, 0, 0, tiled=True)  13 us
    all_to_all x2, starting transfers between devices, over_plane(): parts = lax.all_to_all(part, PLANE, 0, 0, tiled=True)  12.1 us
    all_to_all x2, starting transfers between devices, from_everyone(): return lax.all_to_all(copies, axes, 0, 0, tiled=True)  9.15 us
  transfers between devices with their start and end apart: 34, of which 16 were waited for; matrix products, arithmetic and copies ran while one was open for 14% of the time, Pallas kernels for 0%

profile of v4, /device:TPU:2, one launch (start us, length us, event | category | flops | bytes accessed | tf_op | source)
XLA Modules:
  0.0 234.4 jit_solution(9047044535244067526)
XLA Ops:
  19.7 2.2 collective-permute-start.3
  27.8 2.7 %collective-permute-start.5 = (bf16[4,256,256]{2,1,0:T(8,128)(2,1)S(1)}, bf16[4,256,256]{2,1,0:T(8,128)(2,1)}, u32[]{:S(2)}, u32[]{:S(2)}) collective-permute-start(bf16[4,256,256]{2,1,0:T(8,128)(2,1)S(1)} %constant_dynamic-update-slice_fusion.4), channel_id=1, source_target_pairs={{0,192},{64,0},{128,64},{192,128},{1,193},{65,1},{129,65},{193,129... | collective-permute-start | bytes 1572872 | tf_op jit(solution)/shard_map/ppermute | solution.py:24
  33.2 4.3 %collective-permute-done.12 = bf16[4,256,256]{2,1,0:T(8,128)(2,1)} collective-permute-done((bf16[4,256,256]{2,1,0:T(8,128)(2,1)S(1)}, bf16[4,256,256]{2,1,0:T(8,128)(2,1)}, u32[]{:S(2)}, u32[]{:S(2)}) %collective-permute-start.12) | collective-permute-done | bytes 524320 | tf_op jit(solution)/shard_map/ppermute | solution.py:24
  44.4 2.7 %collective-permute-start.7 = (bf16[2,256,256]{2,1,0:T(8,128)(2,1)S(1)}, bf16[2,256,256]{2,1,0:T(8,128)(2,1)S(1)}, u32[]{:S(2)}, u32[]{:S(2)}) collective-permute-start(bf16[2,256,256]{2,1,0:T(8,128)(2,1)S(1)} %slice.108), channel_id=1, source_target_pairs={{0,192},{64,0},{128,64},{192,128},{1,193},{65,1},{129,65},{193,129... | collective-permute-start | bytes 786440 | tf_op jit(solution)/shard_map/ppermute | solution.py:24
  55.5 3.7 %collective-permute-done.16.inv_other_ref = bf16[4096,256]{1,0:T(8,128)(2,1)} collective-permute-done((bf16[4096,256]{1,0:T(8,128)(2,1)}, bf16[4096,256]{1,0:T(8,128)(2,1)}, u32[]{:S(2)}, u32[]{:S(2)}) %collective-permute-start.16) | collective-permute-done | bytes 2097184 | tf_op jit(solution)/shard_map/ppermute | solution.py:24
  59.2 3.0 %collective-permute-done.8.q_other_ref = bf16[4096,256]{1,0:T(8,128)(2,1)} collective-permute-done((bf16[4096,256]{1,0:T(8,128)(2,1)S(1)}, bf16[4096,256]{1,0:T(8,128)(2,1)}, u32[]{:S(2)}, u32[]{:S(2)}) %collective-permute-start.8) | collective-permute-done | bytes 2097184 | tf_op jit(solution)/shard_map/ppermute | solution.py:24
  62.2 5.3 %all-gather.4.cloned.1.call-done.both_ref = bf16[512,4096]{1,0:T(8,128)(2,1)} async-done(((bf16[512,512]{1,0:T(8,128)(2,1)}), bf16[512,4096]{1,0:T(8,128)(2,1)}) %all-gather.4.cloned.1.call-update) | async-done | bytes 4194320 | tf_op jit(solution)/shard_map/all_gather | solution.py:141
  67.5 2.2 copy-done
  69.7 5.4 %whitened.1 = bf16[512,512]{1,0:T(8,128)(2,1)S(1)} custom-call(s32[1]{0:T(128)} %bitcast.core_ref, f32[512,1]{1,0:T(8,128)S(1)} %copy.71.scale_ref, bf16[512,4096]{1,0:T(8,128)(2,1)S(1)} %copy-done, bf16[4096,256]{1,0:T(8,128)(2,1)S(1)} %bitcast.85, bf16[4096,256]{1,0:T(8,128)(2,1)} %collective-permute-done.8.q_other_ref, ...), custom_call_target="tpu_custom_call" | custom-call | flops 2147483648 | bytes 12582912 | tf_op jit(solution)/shard_map/whitened/pallas_call | solution.py:111
  77.8 11.0 %collective-permute-done.17 = bf16[512,512]{1,0:T(8,128)(2,1)S(1)} collective-permute-done((bf16[512,512]{1,0:T(8,128)(2,1)S(1)}, bf16[512,512]{1,0:T(8,128)(2,1)S(1)}, u32[]{:S(2)}, u32[]{:S(2)}) %collective-permute-start.17) | collective-permute-done | bytes 524320 | tf_op jit(solution)/shard_map/ppermute | solution.py:24
  91.0 3.2 %collective-permute-start.21 = (bf16[512,512]{1,0:T(8,128)(2,1)S(1)}, bf16[512,512]{1,0:T(8,128)(2,1)S(1)}, u32[]{:S(2)}, u32[]{:S(2)}) collective-permute-start(bf16[512,512]{1,0:T(8,128)(2,1)S(1)} %collective-permute-done.17), channel_id=1, source_target_pairs={{0,7},{1,0},{2,1},{3,2},{4,3},{5,4},{6,5},{7,6},{8,15},{9,8},{10,9... | collective-permute-start | bytes 1572872 | tf_op jit(solution)/shard_map/ppermute | solution.py:24
  95.7 9.3 %collective-permute-done.20 = bf16[512,512]{1,0:T(8,128)(2,1)S(1)} collective-permute-done((bf16[512,512]{1,0:T(8,128)(2,1)S(1)}, bf16[512,512]{1,0:T(8,128)(2,1)S(1)}, u32[]{:S(2)}, u32[]{:S(2)}) %collective-permute-start.20) | collective-permute-done | bytes 524320 | tf_op jit(solution)/shard_map/ppermute | solution.py:24
  107.4 13.0 %all_to_all.25 = f32[8,2,128]{2,1,0:T(2,128)S(1)} all-to-all(f32[8,2,128]{2,1,0:T(2,128)S(1)} %broadcast_in_dim.97), channel_id=1, replica_groups=mesh['rows_0'=4,'rows_1'=4,'rows_2'=2,'cols'=8] {'cols'}, dimensions={0} | all-to-all | bytes 16384 | tf_op jit(solution)/shard_map/all_to_all | solution.py:66
  120.3 7.3 %all-to-all-start = ((bf16[16,16,1024]{2,1,0:T(8,128)(2,1)}), bf16[16,16,1024]{2,1,0:T(8,128)(2,1)}, u32[]{:S(2)}, u32[]{:S(2)}) async-start(bf16[16,16,1024]{2,1,0:T(8,128)(2,1)} %bitcast.89), calls=%async_computation | async-start | bytes 1048576 | tf_op jit(solution)/shard_map/all_to_all | solution.py:184
  127.6 2.2 add_convert_fusion
  129.8 7.3 %all-to-all-done = bf16[16,16,1024]{2,1,0:T(8,128)(2,1)} async-done(((bf16[16,16,1024]{2,1,0:T(8,128)(2,1)}), bf16[16,16,1024]{2,1,0:T(8,128)(2,1)}, u32[]{:S(2)}, u32[]{:S(2)}) %all-to-all-start) | async-done | bytes 524320 | tf_op jit(solution)/shard_map/all_to_all | solution.py:184
  137.2 4.8 %all-to-all-start.1 = ((bf16[16,16,1536]{2,1,0:T(8,128)(2,1)}), bf16[16,16,1536]{2,1,0:T(8,128)(2,1)S(1)}, u32[]{:S(2)}, u32[]{:S(2)}) async-start(bf16[16,16,1536]{2,1,0:T(8,128)(2,1)} %bitcast.88), calls=%async_computation.1 | async-start | bytes 1572864 | tf_op jit(solution)/shard_map/all_to_all | solution.py:184
  144.4 9.2 %all-to-all-done.1 = bf16[16,16,1536]{2,1,0:T(8,128)(2,1)S(1)} async-done(((bf16[16,16,1536]{2,1,0:T(8,128)(2,1)}), bf16[16,16,1536]{2,1,0:T(8,128)(2,1)S(1)}, u32[]{:S(2)}, u32[]{:S(2)}) %all-to-all-start.1) | async-done | bytes 786464 | tf_op jit(solution)/shard_map/all_to_all | solution.py:184
  157.7 5.0 %all-to-all-start.3 = ((bf16[16,16,2688]{2,1,0:T(8,128)(2,1)}), bf16[16,16,2688]{2,1,0:T(8,128)(2,1)S(1)}, u32[]{:S(2)}, u32[]{:S(2)}) async-start(bf16[16,16,2688]{2,1,0:T(8,128)(2,1)} %broadcast_in_dim.99), calls=%async_computation.3 | async-start | bytes 2752512 | tf_op jit(solution)/shard_map/all_to_all | solution.py:66
  163.4 17.2 %all-to-all-done.3 = bf16[16,16,2688]{2,1,0:T(8,128)(2,1)S(1)} async-done(((bf16[16,16,2688]{2,1,0:T(8,128)(2,1)}), bf16[16,16,2688]{2,1,0:T(8,128)(2,1)S(1)}, u32[]{:S(2)}, u32[]{:S(2)}) %all-to-all-start.3) | async-done | bytes 1376288 | tf_op jit(solution)/shard_map/all_to_all | solution.py:66
  180.9 19.9 %all-gather.6.cloned.1.call-done = bf16[4096,128]{1,0:T(8,128)(2,1)} async-done(((bf16[512,128]{1,0:T(8,128)(2,1)}), bf16[4096,128]{1,0:T(8,128)(2,1)}) %all-gather.6.cloned.1.call-update) | async-done | bytes 1048592 | tf_op jit(solution)/shard_map/all_gather | solution.py:199
  202.6 4.2 %all-to-all-start.4 = ((f32[16,8,128]{2,1,0:T(8,128)}), f32[16,8,128]{2,1,0:T(8,128)S(1)}, u32[]{:S(2)}, u32[]{:S(2)}) async-start(f32[16,8,128]{2,1,0:T(8,128)} %broadcast_in_dim_broadcast_in_dim_broadcast_in_dim.2), calls=%async_computation.4 | async-start | bytes 131072 | tf_op jit(solution)/shard_map/all_to_all | solution.py:66
  211.4 2.9 %collective-permute-start.24 = (bf16[512,128]{1,0:T(8,128)(2,1)S(1)}, bf16[512,128]{1,0:T(8,128)(2,1)S(1)}, u32[]{:S(2)}, u32[]{:S(2)}) collective-permute-start(bf16[512,128]{1,0:T(8,128)(2,1)S(1)} %convolution_convert_fusion.1), channel_id=1, source_target_pairs={{0,2},{1,3},{2,4},{3,5},{4,6},{5,7},{6,0},{7,1},{8,10},{9,11},{10,... | collective-permute-start | bytes 393224 | tf_op jit(solution)/shard_map/ppermute | solution.py:24
  222.0 2.6 %collective-permute-done.25 = bf16[512,128]{1,0:T(8,128)(2,1)S(1)} collective-permute-done((bf16[512,128]{1,0:T(8,128)(2,1)S(1)}, bf16[512,128]{1,0:T(8,128)(2,1)S(1)}, u32[]{:S(2)}, u32[]{:S(2)}) %collective-permute-start.25) | collective-permute-done | bytes 131104 | tf_op jit(solution)/shard_map/ppermute | solution.py:24
  (149 shorter events, 66.2 us)
Async XLA Ops:
  7.2 60.3 %all-gather.4.cloned.1.call-start = ((), (), s32[]{:S(2)}) async-start(), calls=%async_computation.5 | async-start | bytes 4718592 | tf_op jit(solution)/shard_map/all_gather | solution.py:141
  13.4 8.6 %collective-permute-start.10 = (bf16[256,256]{0,1:T(8,128)(2,1)S(1)}, bf16[256,256]{0,1:T(8,128)(2,1)S(1)}, u32[]{:S(2)}, u32[]{:S(2)}) collective-permute-start(bf16[256,256]{0,1:T(8,128)(2,1)S(1)} %maximum_select_fusion.4), channel_id=1, source_target_pairs={{0,192},{64,0},{128,64},{192,128},{1,193},{65,1},{129,65},{193,129... | collective-permute-start | bytes 393224 | tf_op jit(solution)/shard_map/ppermute | solution.py:24
  22.8 14.7 %collective-permute-start.12 = (bf16[4,256,256]{2,1,0:T(8,128)(2,1)S(1)}, bf16[4,256,256]{2,1,0:T(8,128)(2,1)}, u32[]{:S(2)}, u32[]{:S(2)}) collective-permute-start(bf16[4,256,256]{2,1,0:T(8,128)(2,1)S(1)} %constant_dynamic-update-slice_fusion), channel_id=1, source_target_pairs={{0,16},{16,32},{32,48},{48,0},{1,17},{17,33},{33,49},{49,1},{2,18}... | collective-permute-start | bytes 1572872 | tf_op jit(solution)/shard_map/ppermute | solution.py:24
  24.4 15.7 %collective-permute-start.13 = (bf16[4,256,256]{2,1,0:T(8,128)(2,1)S(1)}, bf16[4,256,256]{2,1,0:T(8,128)(2,1)}, u32[]{:S(2)}, u32[]{:S(2)}) collective-permute-start(bf16[4,256,256]{2,1,0:T(8,128)(2,1)S(1)} %constant_dynamic-update-slice_fusion), channel_id=1, source_target_pairs={{0,48},{16,0},{32,16},{48,32},{1,49},{17,1},{33,17},{49,33},{2,50}... | collective-permute-start | bytes 1572872 | tf_op jit(solution)/shard_map/ppermute | solution.py:24
  27.2 14.4 %collective-permute-start.4 = (bf16[4,256,256]{2,1,0:T(8,128)(2,1)S(1)}, bf16[4,256,256]{2,1,0:T(8,128)(2,1)}, u32[]{:S(2)}, u32[]{:S(2)}) collective-permute-start(bf16[4,256,256]{2,1,0:T(8,128)(2,1)S(1)} %constant_dynamic-update-slice_fusion.4), channel_id=1, source_target_pairs={{0,64},{64,128},{128,192},{192,0},{1,65},{65,129},{129,193},{193,1... | collective-permute-start | bytes 1572872 | tf_op jit(solution)/shard_map/ppermute | solution.py:24
  27.8 15.7 %collective-permute-start.5 = (bf16[4,256,256]{2,1,0:T(8,128)(2,1)S(1)}, bf16[4,256,256]{2,1,0:T(8,128)(2,1)}, u32[]{:S(2)}, u32[]{:S(2)}) collective-permute-start(bf16[4,256,256]{2,1,0:T(8,128)(2,1)S(1)} %constant_dynamic-update-slice_fusion.4), channel_id=1, source_target_pairs={{0,192},{64,0},{128,64},{192,128},{1,193},{65,1},{129,65},{193,129... | collective-permute-start | bytes 1572872 | tf_op jit(solution)/shard_map/ppermute | solution.py:24
  38.5 14.7 %collective-permute-start.14 = (bf16[2,256,256]{2,1,0:T(8,128)(2,1)S(1)}, bf16[2,256,256]{2,1,0:T(8,128)(2,1)S(1)}, u32[]{:S(2)}, u32[]{:S(2)}) collective-permute-start(bf16[2,256,256]{2,1,0:T(8,128)(2,1)S(1)} %slice.110), channel_id=1, source_target_pairs={{0,16},{16,32},{32,48},{48,0},{1,17},{17,33},{33,49},{49,1},{2,18}... | collective-permute-start | bytes 786440 | tf_op jit(solution)/shard_map/ppermute | solution.py:24
  41.0 12.9 %collective-permute-start.15 = (bf16[2,256,256]{2,1,0:T(8,128)(2,1)S(1)}, bf16[2,256,256]{2,1,0:T(8,128)(2,1)S(1)}, u32[]{:S(2)}, u32[]{:S(2)}) collective-permute-start(bf16[2,256,256]{2,1,0:T(8,128)(2,1)S(1)} %slice.111), channel_id=1, source_target_pairs={{0,48},{16,0},{32,16},{48,32},{1,49},{17,1},{33,17},{49,33},{2,50}... | collective-permute-start | bytes 786440 | tf_op jit(solution)/shard_map/ppermute | solution.py:24
  42.6 12.1 %collective-permute-start.6 = (bf16[2,256,256]{2,1,0:T(8,128)(2,1)S(1)}, bf16[2,256,256]{2,1,0:T(8,128)(2,1)S(1)}, u32[]{:S(2)}, u32[]{:S(2)}) collective-permute-start(bf16[2,256,256]{2,1,0:T(8,128)(2,1)S(1)} %slice.107), channel_id=1, source_target_pairs={{0,64},{64,128},{128,192},{192,0},{1,65},{65,129},{129,193},{193,1... | collective-permute-start | bytes 786440 | tf_op jit(solution)/shard_map/ppermute | solution.py:24
  44.4 10.3 %collective-permute-start.7 = (bf16[2,256,256]{2,1,0:T(8,128)(2,1)S(1)}, bf16[2,256,256]{2,1,0:T(8,128)(2,1)S(1)}, u32[]{:S(2)}, u32[]{:S(2)}) collective-permute-start(bf16[2,256,256]{2,1,0:T(8,128)(2,1)S(1)} %slice.108), channel_id=1, source_target_pairs={{0,192},{64,0},{128,64},{192,128},{1,193},{65,1},{129,65},{193,129... | collective-permute-start | bytes 786440 | tf_op jit(solution)/shard_map/ppermute | solution.py:24
  75.2 13.6 %collective-permute-start.17 = (bf16[512,512]{1,0:T(8,128)(2,1)S(1)}, bf16[512,512]{1,0:T(8,128)(2,1)S(1)}, u32[]{:S(2)}, u32[]{:S(2)}) collective-permute-start(bf16[512,512]{1,0:T(8,128)(2,1)S(1)} %whitened.1), channel_id=1, source_target_pairs={{0,7},{1,0},{2,1},{3,2},{4,3},{5,4},{6,5},{7,6},{8,15},{9,8},{10,9... | collective-permute-start | bytes 1572872 | tf_op jit(solution)/shard_map/ppermute | solution.py:24
  76.6 14.4 %collective-permute-start.19 = (bf16[512,512]{1,0:T(8,128)(2,1)S(1)}, bf16[512,512]{1,0:T(8,128)(2,1)S(1)}, u32[]{:S(2)}, u32[]{:S(2)}) collective-permute-start(bf16[512,512]{1,0:T(8,128)(2,1)S(1)} %whitened.1), channel_id=1, source_target_pairs={{0,1},{1,2},{2,3},{3,4},{4,5},{5,6},{6,7},{7,0},{8,9},{9,10},{10,1... | collective-permute-start | bytes 1572872 | tf_op jit(solution)/shard_map/ppermute | solution.py:24
  91.0 13.9 %collective-permute-start.20 = (bf16[512,512]{1,0:T(8,128)(2,1)S(1)}, bf16[512,512]{1,0:T(8,128)(2,1)S(1)}, u32[]{:S(2)}, u32[]{:S(2)}) collective-permute-start(bf16[512,512]{1,0:T(8,128)(2,1)S(1)} %collective-permute-done.19), channel_id=1, source_target_pairs={{0,1},{1,2},{2,3},{3,4},{4,5},{5,6},{6,7},{7,0},{8,9},{9,10},{10,1... | collective-permute-start | bytes 1572872 | tf_op jit(solution)/shard_map/ppermute | solution.py:24
  91.0 13.9 %collective-permute-start.21 = (bf16[512,512]{1,0:T(8,128)(2,1)S(1)}, bf16[512,512]{1,0:T(8,128)(2,1)S(1)}, u32[]{:S(2)}, u32[]{:S(2)}) collective-permute-start(bf16[512,512]{1,0:T(8,128)(2,1)S(1)} %collective-permute-done.17), channel_id=1, source_target_pairs={{0,7},{1,0},{2,1},{3,2},{4,3},{5,4},{6,5},{7,6},{8,15},{9,8},{10,9... | collective-permute-start | bytes 1572872 | tf_op jit(solution)/shard_map/ppermute | solution.py:24
  107.2 20.5 %collective-permute-start.22 = (bf16[256,1536]{1,0:T(8,128)(2,1)}, bf16[256,1536]{1,0:T(8,128)(2,1)}, u32[]{:S(2)}, u32[]{:S(2)}) collective-permute-start(bf16[256,1536]{1,0:T(8,128)(2,1)} %dynamic-slice_convert_fusion), channel_id=1, source_target_pairs={{0,8},{8,0},{1,9},{9,1},{2,10},{10,2},{3,11},{11,3},{4,12},{12,4},... | collective-permute-start | bytes 2359304 | tf_op jit(solution)/shard_map/ppermute | solution.py:24
  120.3 16.8 %all-to-all-start = ((bf16[16,16,1024]{2,1,0:T(8,128)(2,1)}), bf16[16,16,1024]{2,1,0:T(8,128)(2,1)}, u32[]{:S(2)}, u32[]{:S(2)}) async-start(bf16[16,16,1024]{2,1,0:T(8,128)(2,1)} %bitcast.89), calls=%async_computation | async-start | bytes 1048576 | tf_op jit(solution)/shard_map/all_to_all | solution.py:184
  137.2 16.5 %all-to-all-start.1 = ((bf16[16,16,1536]{2,1,0:T(8,128)(2,1)}), bf16[16,16,1536]{2,1,0:T(8,128)(2,1)S(1)}, u32[]{:S(2)}, u32[]{:S(2)}) async-start(bf16[16,16,1536]{2,1,0:T(8,128)(2,1)} %bitcast.88), calls=%async_computation.1 | async-start | bytes 1572864 | tf_op jit(solution)/shard_map/all_to_all | solution.py:184
  157.7 22.9 %all-to-all-start.3 = ((bf16[16,16,2688]{2,1,0:T(8,128)(2,1)}), bf16[16,16,2688]{2,1,0:T(8,128)(2,1)S(1)}, u32[]{:S(2)}, u32[]{:S(2)}) async-start(bf16[16,16,2688]{2,1,0:T(8,128)(2,1)} %broadcast_in_dim.99), calls=%async_computation.3 | async-start | bytes 2752512 | tf_op jit(solution)/shard_map/all_to_all | solution.py:66
  162.6 38.2 %all-gather.6.cloned.1.call-start = ((), (), s32[]{:S(2)}) async-start(), calls=%async_computation.6 | async-start | bytes 1179648 | tf_op jit(solution)/shard_map/all_gather | solution.py:199
  180.7 26.1 %collective-permute-start.23 = (bf16[256,2560]{1,0:T(8,128)(2,1)S(1)}, bf16[256,2560]{1,0:T(8,128)(2,1)}, u32[]{:S(2)}, u32[]{:S(2)}) collective-permute-start(bf16[256,2560]{1,0:T(8,128)(2,1)S(1)} %bitcast.86), channel_id=1, source_target_pairs={{0,8},{8,0},{1,9},{9,1},{2,10},{10,2},{3,11},{11,3},{4,12},{12,4},... | collective-permute-start | bytes 3932168 | tf_op jit(solution)/shard_map/ppermute | solution.py:24
  202.6 16.9 %all-to-all-start.4 = ((f32[16,8,128]{2,1,0:T(8,128)}), f32[16,8,128]{2,1,0:T(8,128)S(1)}, u32[]{:S(2)}, u32[]{:S(2)}) async-start(f32[16,8,128]{2,1,0:T(8,128)} %broadcast_in_dim_broadcast_in_dim_broadcast_in_dim.2), calls=%async_computation.4 | async-start | bytes 131072 | tf_op jit(solution)/shard_map/all_to_all | solution.py:66
  211.4 10.6 %collective-permute-start.24 = (bf16[512,128]{1,0:T(8,128)(2,1)S(1)}, bf16[512,128]{1,0:T(8,128)(2,1)S(1)}, u32[]{:S(2)}, u32[]{:S(2)}) collective-permute-start(bf16[512,128]{1,0:T(8,128)(2,1)S(1)} %convolution_convert_fusion.1), channel_id=1, source_target_pairs={{0,2},{1,3},{2,4},{3,5},{4,6},{5,7},{6,0},{7,1},{8,10},{9,11},{10,... | collective-permute-start | bytes 393224 | tf_op jit(solution)/shard_map/ppermute | solution.py:24
  214.6 10.1 %collective-permute-start.25 = (bf16[512,128]{1,0:T(8,128)(2,1)S(1)}, bf16[512,128]{1,0:T(8,128)(2,1)S(1)}, u32[]{:S(2)}, u32[]{:S(2)}) collective-permute-start(bf16[512,128]{1,0:T(8,128)(2,1)S(1)} %convolution_convert_fusion), channel_id=1, source_target_pairs={{0,6},{1,7},{2,0},{3,1},{4,2},{5,3},{6,4},{7,5},{8,14},{9,15},{10,... | collective-permute-start | bytes 393224 | tf_op jit(solution)/shard_map/ppermute | solution.py:24
  216.5 10.3 %collective-permute-start.26 = (bf16[512,128]{1,0:T(8,128)(2,1)S(1)}, bf16[512,128]{1,0:T(8,128)(2,1)S(1)}, u32[]{:S(2)}, u32[]{:S(2)}) collective-permute-start(bf16[512,128]{1,0:T(8,128)(2,1)S(1)} %convolution_convert_fusion.2), channel_id=1, source_target_pairs={{0,7},{1,0},{2,1},{3,2},{4,3},{5,4},{6,5},{7,6},{8,15},{9,8},{10,9... | collective-permute-start | bytes 393224 | tf_op jit(solution)/shard_map/ppermute | solution.py:24
  (15 other events, 93.4 us)
Sparse Core Ops, SparseCore 0:
  9.8 57.6 all-gather.3
  165.8 34.9 all-gather.5
